TPU v7x, 32 devices: a whole 2x2x4 slice. The times are simulated.
32 devices in a mesh: dp: 4 (over y, core), tensor: 8 (over z, x).
Axes of the slice: x: 2, y: 2, z: 4, core: 2. Of those that a mesh axis runs over, the one named last changes fastest.
Arguments:
- ref_hidden: bfloat16 [1152, 4608], P('dp', 'tensor'), may hold values from -6 to 6
- pol_hidden: bfloat16 [1152, 4608], P('dp', 'tensor'), may hold values from -6 to 6
- readout: bfloat16 [1152, 4608], P('dp', 'tensor'), may hold values from -0.019897461 to 0.019897461
- lengths: int32 [12], P('dp'), may hold values from 16 to 96, as said below
- pairing: int32 [12], replicated, may hold values from 0 to 11, each once
- pre_gain: float32 [4608], replicated, may hold values from 0.25 to 1.75
- post_gain: float32 [4608], replicated, may hold values from 0.25 to 1.75
- w_query: bfloat16 [4608, 4096], P('dp', 'tensor'), may hold values from -0.09375 to 0.09375
- w_key: bfloat16 [4608, 2048], P('dp', 'tensor'), may hold values from -3 to 3
- value_projection: bfloat16 [4608, 2048], P('dp', 'tensor'), may hold values from -0.09375 to 0.09375
- w_out: bfloat16 [4608, 4096], P('dp', 'tensor'), may hold values from -0.09375 to 0.09375
- a_query: bfloat16 [4608, 64], P('dp'), may hold values from -0.09375 to 0.09375
- a_value: bfloat16 [4608, 64], P('dp'), may hold values from -0.09375 to 0.09375
- query_second_factor: bfloat16 [64, 4096], P(None, 'tensor'), may hold values from -0.75 to 0.75
- value_second_factor: bfloat16 [64, 2048], P(None, 'tensor'), may hold values from -0.75 to 0.75
Outputs:
- policy_out: bfloat16 [1152, 4608], P('dp', 'tensor')
- reference_out: bfloat16 [1152, 4608], P('dp', 'tensor')
- dpo_loss: float32 [], replicated
- grad_hidden: bfloat16 [1152, 4608], P('dp', 'tensor')
- grad_a: float32 [4608, 128], P('dp')
- query_factor_gradient: float32 [64, 4096], P(None, 'tensor')
- value_factor_gradient: float32 [64, 2048], P(None, 'tensor')
Inputs may be any that keep to these rules, and one draw needn't show every extreme that they name: `lengths`: every sequence has at least one valid token and some sequence is full. `pairing`: entries 2k and 2k + 1 name the chosen and the rejected sequence of pair k; every sequence appears once.
All inputs are finite; a program needn't handle non-finite values.
Results may differ from a plain program's by a relative error of at most 0.0233.
The roundings to bfloat16 on the way count: a program that leaves them out, or rounds other values in their place, can miss the bound.
Values may be sent and summed in bfloat16 or wider, within the bound.
A program may use at most 128 MiB of HBM per device.

v0:
```python
import jax
import jax.numpy as jnp
from jax import lax
from jax.experimental import pallas as pl
from jax.experimental.pallas import tpu as pltpu
from jax.sharding import PartitionSpec as P

MODEL_WIDTH = 4608
HQ = 32
HEAD_SIZE = 128


NORM_EPS = 1e-06
SOFT_CAP = 50.0
ADAPTER_SCALE = 0.5
DPO_BETA = 0.5
LOSS_SCALE = 256.0
ROPE_BASE = 10000.0


def query_scale():
    return float(MODEL_WIDTH // HQ) ** (-0.5)


def apply_rotation(value_rows, direction):
    length = value_rows.shape[1]
    head_depth = value_rows.shape[3]
    middle = head_depth // 2
    spacing = ROPE_BASE ** (-2.0 * jnp.arange(middle, dtype=jnp.float32) / head_depth)
    angles = jnp.arange(length, dtype=jnp.float32)[:, None] * spacing[None, :]
    cosine = jnp.cos(angles)[None, :, None, :]
    sine_part = direction * jnp.sin(angles)[None, :, None, :]
    leading = value_rows[..., :middle]
    trailing = value_rows[..., middle:]
    return jnp.concatenate(
        [leading * cosine - trailing * sine_part, trailing * cosine + leading * sine_part], axis=-1
    )


def allowed_mask(lengths, length):
    places = jnp.arange(length)
    causal = places[None, :] <= places[:, None]
    living = places[None, :] < lengths[:, None]
    return causal[None, None, None, :, :] & living[:, None, None, None, :]


def attend(query_rows, rotated_keys, value_rows, lengths):
    seqs_here, length, q_heads, head_depth = query_rows.shape
    kv_heads = rotated_keys.shape[2]
    grouped_heads = query_rows.reshape(seqs_here, length, kv_heads, q_heads // kv_heads, head_depth)
    scores = (
        jnp.einsum(
            "sqkgd,spkd->skgqp", grouped_heads, rotated_keys, preferred_element_type=jnp.float32
        )
        * query_scale()
    )
    capped = SOFT_CAP * jnp.tanh(scores / SOFT_CAP)
    allowed = allowed_mask(lengths, length)
    weights = jnp.where(allowed, jnp.exp(capped), 0.0)
    probabilities = weights / jnp.sum(weights, axis=-1, keepdims=True)
    probs_low = probabilities.astype(jnp.bfloat16)
    mixed_out = jnp.einsum(
        "skgqp,spkd->sqkgd", probs_low, value_rows, preferred_element_type=jnp.float32
    )
    return (
        mixed_out.astype(jnp.bfloat16).reshape(seqs_here, length, q_heads, head_depth),
        probs_low,
        probabilities,
        capped,
    )


def attend_back(grad_mixed, query_rows, rotated_keys, value_rows, probs_low, probabilities, capped):
    seqs_here, length, q_heads, head_depth = query_rows.shape
    kv_heads = rotated_keys.shape[2]
    shape_five = (seqs_here, length, kv_heads, q_heads // kv_heads, head_depth)
    grouped_heads = query_rows.reshape(shape_five)
    grad_grouped = grad_mixed.reshape(shape_five)
    grad_probs = jnp.einsum(
        "sqkgd,spkd->skgqp", grad_grouped, value_rows, preferred_element_type=jnp.float32
    )
    value_rows_gradient = jnp.einsum(
        "skgqp,sqkgd->spkd", probs_low, grad_grouped, preferred_element_type=jnp.float32
    )
    centered = grad_probs - jnp.sum(grad_probs * probabilities, axis=-1, keepdims=True)
    grad_scores = (
        probabilities * centered * (1.0 - (capped / SOFT_CAP) ** 2) * query_scale()
    ).astype(jnp.bfloat16)
    query_rows_gradient = jnp.einsum(
        "skgqp,spkd->sqkgd", grad_scores, rotated_keys, preferred_element_type=jnp.float32
    ).reshape(seqs_here, length, q_heads, head_depth)
    key_rows_gradient = jnp.einsum(
        "skgqp,sqkgd->spkd", grad_scores, grouped_heads, preferred_element_type=jnp.float32
    )
    return (query_rows_gradient, key_rows_gradient, value_rows_gradient)


MESH = pl.DeviceIdType.MESH
VMEM_GRANT = 60 * 2**20


def grid_of(axis, count):
    if axis == "dp":
        inner = 2 if count % 2 == 0 else 1
    else:
        inner = 1
        while (inner * 2) ** 2 <= count and count % (inner * 2) == 0:
            inner *= 2
    return count // inner, inner


def row_chunk(rows):
    for size in (48, 32, 16):
        if rows % size == 0:
            return size
    return rows


def piece_rows(rows):
    for size in range(96, 0, -16):
        if rows % size == 0:
            return size
    return rows


class Place:
    def __init__(self, axis, count):
        self.axis = axis
        self.outer, self.inner = grid_of(axis, count)
        rank = lax.axis_index(axis)
        self.a = lax.div(rank, self.inner)
        self.b = lax.rem(rank, self.inner)
        self.rank = rank

    def out_at(self, j):
        return lax.rem(self.a + j + self.outer, self.outer)

    def in_at(self, k):
        return lax.rem(self.b + k + self.inner, self.inner)

    def slot(self, j, k):
        return self.out_at(j) * self.inner + self.in_at(k)

    def peers(self):
        return [self.slot(j, 0) for j in range(1, self.outer)] + [
            self.slot(0, k) for k in range(1, self.inner)
        ]


def remote(src, dst, send_sem, recv_sem, axis, rank):
    return pltpu.make_async_remote_copy(
        src_ref=src,
        dst_ref=dst,
        send_sem=send_sem,
        recv_sem=recv_sem,
        device_id={axis: rank},
        device_id_type=MESH,
    )


def communicate(name, number, counts, gathers=(), reduces=(), gain=None):
    places_used = sorted({axis for _, axis, _ in gathers} | ({"tensor"} if reduces else set()))
    tensor_count = counts["tensor"]
    operands, in_specs, out_shapes, out_specs, scratch = [], [], [], [], []
    vmem = pl.BlockSpec(memory_space=pltpu.VMEM)
    plan = []
    for array, axis, kind in gathers:
        operands.append(array)
        in_specs.append(vmem)
        whole = (counts[axis],) + array.shape
        outer, inner = grid_of(axis, counts[axis])
        entry = {"axis": axis, "kind": kind, "x": len(operands) - 1}
        if kind in ("vmem", "hbm"):
            entry["out"] = len(out_shapes)
            out_shapes.append(jax.ShapeDtypeStruct(whole, array.dtype))
            out_specs.append(vmem if kind == "vmem" else pl.BlockSpec(memory_space=pl.ANY))
        else:
            entry["held"] = len(scratch)
            scratch.append(pltpu.VMEM(whole, array.dtype))
            entry["out"] = len(out_shapes)
            out_shapes.append(
                jax.ShapeDtypeStruct((array.shape[0], array.shape[1] * counts[axis]), jnp.bfloat16)
            )
            out_specs.append(vmem)
            if kind == "norm":
                out_shapes.append(jax.ShapeDtypeStruct((array.shape[0], 1), jnp.float32))
                out_specs.append(vmem)
                entry["gain"] = len(operands)
                operands.append(gain.reshape(1, -1))
                in_specs.append(vmem)
        entry["sems"] = len(scratch)
        size = piece_rows(array.shape[0]) if "held" in entry else array.shape[0]
        entry["size"], entry["pieces"] = size, array.shape[0] // size
        n_outer = max(outer - 1, 1) * entry["pieces"]
        n_inner = max(outer * (inner - 1), 1) * entry["pieces"]
        scratch += [
            pltpu.SemaphoreType.DMA((n_outer,)),
            pltpu.SemaphoreType.DMA((n_outer,)),
            pltpu.SemaphoreType.DMA((n_inner,)),
            pltpu.SemaphoreType.DMA((n_inner,)),
            pltpu.SemaphoreType.DMA,
        ]
        plan.append(entry)
    sums = []
    for array in reduces:
        rows, width = array.shape
        outer, inner = grid_of("tensor", tensor_count)
        part = width // tensor_count
        size = piece_rows(rows)
        pieces = rows // size
        n_inner = max(outer * (inner - 1), 1)
        sums.append(
            {
                "x": len(operands),
                "out": len(out_shapes),
                "scratch": len(scratch),
                "size": size,
                "pieces": pieces,
            }
        )
        operands.append(array)
        in_specs.append(vmem)
        out_shapes.append(jax.ShapeDtypeStruct((rows, part), jnp.float32))
        out_specs.append(vmem)
        scratch += [
            pltpu.VMEM((tensor_count, rows, part), array.dtype),
            pltpu.VMEM((n_inner, rows, part), array.dtype),
            pltpu.VMEM((outer, rows, part), array.dtype),
            pltpu.VMEM((outer, rows, part), array.dtype),
            pltpu.SemaphoreType.DMA((n_inner * pieces,)),
            pltpu.SemaphoreType.DMA((n_inner * pieces,)),
            pltpu.SemaphoreType.DMA((outer * pieces,)),
            pltpu.SemaphoreType.DMA((outer * pieces,)),
        ]
    n_in, n_out = len(operands), len(out_shapes)

    def kernel(*refs):
        ins, outs, work = refs[:n_in], refs[n_in : n_in + n_out], refs[n_in + n_out :]
        places = {axis: Place(axis, counts[axis]) for axis in places_used}
        barrier = pltpu.get_barrier_semaphore()
        total = 0
        for axis, place in places.items():
            for peer in place.peers():
                pl.semaphore_signal(barrier, inc=1, device_id={axis: peer}, device_id_type=MESH)
                total += 1
        pl.semaphore_wait(barrier, total)
        for entry in plan:
            place = places[entry["axis"]]
            x = ins[entry["x"]]
            held = work[entry["held"]] if "held" in entry else outs[entry["out"]]
            so, ro, si, ri, own_sem = work[entry["sems"] : entry["sems"] + 5]
            entry["far"], entry["near"] = [], []
            mine = held.at[place.rank]
            for c in range(entry["pieces"]):
                rows = pl.ds(c * entry["size"], entry["size"])
                for j in range(1, place.outer):
                    at = c * (place.outer - 1) + j - 1
                    copy = remote(
                        x.at[rows],
                        mine.at[rows],
                        so.at[at],
                        ro.at[at],
                        place.axis,
                        place.slot(j, 0),
                    )
                    copy.start()
                    entry["far"].append(copy)
                for k in range(1, place.inner):
                    at = c * place.outer * (place.inner - 1) + k - 1
                    copy = remote(
                        x.at[rows],
                        mine.at[rows],
                        si.at[at],
                        ri.at[at],
                        place.axis,
                        place.slot(0, k),
                    )
                    copy.start()
                    entry["near"].append(copy)
            entry["own"] = pltpu.make_async_copy(x, mine, own_sem)
            entry["own"].start()
        for item in sums:
            place = places["tensor"]
            x = ins[item["x"]]
            stage, near_box, outgoing, far_box, si, ri, so, ro = work[
                item["scratch"] : item["scratch"] + 8
            ]
            part = stage.shape[2]
            size = row_chunk(item["size"])
            n_near = place.outer * (place.inner - 1)
            item["near"], item["far"] = {}, {}
            for c in range(item["pieces"]):

                @pl.loop(0, item["size"] // size)
                def _(step, c=c, x=x, stage=stage, part=part, size=size, item=item):
                    at = pl.ds(pl.multiple_of(c * item["size"] + step * size, size), size)
                    for n in range(tensor_count):
                        stage[n, at, :] = x[at, n * part : (n + 1) * part]

                rows = pl.ds(c * item["size"], item["size"])
                for j in [*range(1, place.outer), 0]:
                    for k in range(1, place.inner):
                        at = j * (place.inner - 1) + k - 1
                        copy = remote(
                            stage.at[place.slot(j, k), rows],
                            near_box.at[at, rows],
                            si.at[c * n_near + at],
                            ri.at[c * n_near + at],
                            "tensor",
                            place.slot(0, k),
                        )
                        copy.start()
                        item["near"][c, j, k] = copy
        for item in sums:
            place = places["tensor"]
            out = outs[item["out"]]
            stage, near_box, outgoing, far_box, si, ri, so, ro = work[
                item["scratch"] : item["scratch"] + 8
            ]
            size = row_chunk(item["size"])
            for c in range(item["pieces"]):
                rows = pl.ds(c * item["size"], item["size"])
                for j in [*range(1, place.outer), 0]:
                    for k in range(1, place.inner):
                        item["near"][c, j, k].wait_recv()

                    @pl.loop(0, item["size"] // size)
                    def _(step, c=c, j=j, item=item, size=size):
                        at = pl.ds(pl.multiple_of(c * item["size"] + step * size, size), size)
                        value = stage[place.slot(j, 0), at, :].astype(jnp.float32)
                        for k in range(1, place.inner):
                            value += near_box[j * (place.inner - 1) + k - 1, at, :].astype(
                                jnp.float32
                            )
                        if j:
                            outgoing[j, at, :] = value.astype(outgoing.dtype)
                        else:
                            out[at, :] = value

                    if j:
                        copy = remote(
                            outgoing.at[j, rows],
                            far_box.at[j, rows],
                            so.at[c * place.outer + j],
                            ro.at[c * place.outer + j],
                            "tensor",
                            place.slot(j, 0),
                        )
                        copy.start()
                        item["far"][c, j] = copy
        for entry in sorted(plan, key=lambda entry: "held" not in entry):
            place = places[entry["axis"]]
            held = work[entry["held"]] if "held" in entry else outs[entry["out"]]
            so, ro, si, ri, own_sem = work[entry["sems"] : entry["sems"] + 5]
            for c in range(entry["pieces"]):
                rows = pl.ds(c * entry["size"], entry["size"])
                for j in range(1, place.outer):
                    entry["far"][c * (place.outer - 1) + j - 1].wait_recv()
                    block = held.at[place.slot(-j, 0), rows]
                    for k in range(1, place.inner):
                        at = (c * place.outer + j) * (place.inner - 1) + k - 1
                        copy = remote(
                            block, block, si.at[at], ri.at[at], place.axis, place.slot(0, k)
                        )
                        copy.start()
                        entry["near"].append(copy)
        for entry in plan:
            if "held" in entry:
                finish(entry, ins, outs, work[entry["held"]])
        for item in sums:
            out = outs[item["out"]]
            far_box = work[item["scratch"] + 3]
            size = row_chunk(item["size"])
            outer = places["tensor"].outer
            for c in range(item["pieces"]):
                for j in range(1, outer):
                    item["far"][c, j].wait_recv()

                @pl.loop(0, item["size"] // size)
                def _(step, c=c, out=out, far_box=far_box, size=size, item=item):
                    at = pl.ds(pl.multiple_of(c * item["size"] + step * size, size), size)
                    value = out[at, :]
                    for j in range(1, outer):
                        value += far_box[j, at, :].astype(jnp.float32)
                    out[at, :] = value

            for copy in [*item["near"].values(), *item["far"].values()]:
                copy.wait_send()
        for entry in plan:
            if "held" not in entry:
                for copy in entry["near"]:
                    copy.wait_recv()
                entry["own"].wait()
            for copy in entry["near"] + entry["far"]:
                copy.wait_send()

    def finish(entry, ins, outs, held):
        for copy in entry["near"]:
            copy.wait_recv()
        entry["own"].wait()
        count, rows, part = held.shape
        out = outs[entry["out"]]
        size = row_chunk(rows)

        @pl.loop(0, rows // size)
        def _(step):
            at = pl.ds(pl.multiple_of(step * size, size), size)
            if entry["kind"] == "rows":
                for n in range(count):
                    out[at, n * part : (n + 1) * part] = held[n, at, :].astype(out.dtype)
                return
            square = jnp.zeros((size, part), jnp.float32)
            for n in range(count):
                value = held[n, at, :].astype(jnp.float32)
                square += value * value
            scale = lax.rsqrt(
                jnp.sum(square, axis=1, keepdims=True) / (count * part) + NORM_EPS
            )
            outs[entry["out"] + 1][at, :] = scale
            gain_ref = ins[entry["gain"]]
            for n in range(count):
                cols = slice(n * part, (n + 1) * part)
                value = held[n, at, :].astype(jnp.float32)
                out[at, cols] = (value * scale * gain_ref[:, cols]).astype(out.dtype)

    return pl.pallas_call(
        kernel,
        name=name,
        out_shape=out_shapes,
        in_specs=in_specs,
        out_specs=out_specs,
        scratch_shapes=scratch,
        compiler_params=pltpu.CompilerParams(
            collective_id=number, has_side_effects=True, vmem_limit_bytes=VMEM_GRANT
        ),
    )(*operands)


def body(
    ref_hidden,
    pol_hidden,
    readout,
    lengths,
    pairing,
    pre_gain,
    post_gain,
    w_query,
    w_key,
    value_projection,
    w_out,
    a_query,
    a_value,
    query_second_factor,
    value_second_factor,
):
    f32, bf16 = jnp.float32, jnp.bfloat16
    tok_rows, part_width = pol_hidden.shape
    seqs_here = lengths.shape[0]
    length = tok_rows // seqs_here
    tensor_rank = lax.axis_index("tensor")
    data_rank = lax.axis_index("dp")
    counts = {"dp": lax.axis_size("dp"), "tensor": lax.axis_size("tensor")}
    all_seqs = seqs_here * counts["dp"]
    full_width = part_width * counts["tensor"]
    rank_size = query_second_factor.shape[0]
    rows_contraction = (((0,), (0,)), ((), ()))
    contract_cols = (((1,), (1,)), ((), ()))

    def dot(a, b, dims=(((1,), (0,)), ((), ()))):
        return lax.dot_general(a, b, dims, preferred_element_type=f32)

    pre_local = lax.dynamic_slice_in_dim(pre_gain, tensor_rank * part_width, part_width)
    post_local = lax.dynamic_slice_in_dim(post_gain, tensor_rank * part_width, part_width)
    hidden = jnp.concatenate([ref_hidden, pol_hidden], axis=0)
    gathered = communicate(
        "gather_inputs",
        1,
        counts,
        gathers=[
            (jnp.concatenate([a_query, a_value], axis=1), "dp", "hbm"),
            (w_query, "dp", "hbm"),
            (hidden, "tensor", "norm"),
            (w_key, "dp", "hbm"),
            (value_projection, "dp", "hbm"),
            (w_out, "dp", "hbm"),
        ],
        gain=pre_gain,
    )
    a_both, w_query_all, normed, pre_scale, w_key_all, w_value_all, w_out_all = [
        v.reshape(-1, v.shape[-1]) for v in gathered
    ]
    pol_normed = normed[tok_rows:]
    pol_scale = pre_scale[tok_rows:]
    low_rank_update = dot(pol_normed, a_both).astype(bf16)
    query_rows = dot(normed, w_query_all)
    keys_before_rotation = dot(normed, w_key_all)
    value_rows = dot(normed, w_value_all)
    added_query = ADAPTER_SCALE * dot(low_rank_update[:, :rank_size], query_second_factor)
    added_value = ADAPTER_SCALE * dot(low_rank_update[:, rank_size:], value_second_factor)
    none = ((tok_rows, 0), (0, 0))
    query_rows = query_rows + jnp.pad(added_query, none)
    value_rows = value_rows + jnp.pad(added_value, none)
    q_heads = query_rows.shape[1] // HEAD_SIZE
    kv_heads = value_rows.shape[1] // HEAD_SIZE
    both = 2 * seqs_here
    query_rows = apply_rotation(
        query_rows.reshape(both, length, q_heads, HEAD_SIZE), 1.0
    ).astype(bf16)
    rotated_keys = apply_rotation(
        keys_before_rotation.reshape(both, length, kv_heads, HEAD_SIZE), 1.0
    ).astype(bf16)
    value_rows = value_rows.reshape(both, length, kv_heads, HEAD_SIZE).astype(bf16)
    mixed_out, probs_low, probabilities, capped = attend(
        query_rows, rotated_keys, value_rows, jnp.concatenate([lengths, lengths])
    )
    head_terms = dot(
        mixed_out.reshape(2 * tok_rows, q_heads * HEAD_SIZE), w_out_all, contract_cols
    ).astype(bf16)
    (summed_both,) = communicate("scatter_out", 2, counts, reduces=[head_terms])
    readout_wide = readout.astype(f32)
    living = (jnp.arange(length)[None, :] < lengths[:, None]).astype(f32)
    weighted = post_local * readout_wide
    shaped = summed_both.reshape(2, tok_rows, part_width)
    hidden_wide = hidden.astype(f32).reshape(2, tok_rows, part_width)
    stats = jnp.concatenate(
        [
            jnp.sum(shaped * shaped, axis=2),
            jnp.sum(shaped * weighted, axis=2),
            jnp.sum(hidden_wide * readout_wide, axis=2),
            jnp.zeros((2, tok_rows), f32),
        ],
        axis=0,
    )
    (stats_all,) = communicate("token_sums", 3, counts, gathers=[(stats, "tensor", "vmem")])
    stats = jnp.sum(stats_all, axis=0)
    post_scale = lax.rsqrt(stats[0:2] / full_width + NORM_EPS)
    token_scores = (stats[4:6] + post_scale * stats[2:4]).reshape(2, seqs_here, length) * living
    mine = jnp.sum(token_scores, axis=2)
    mine = jnp.pad(mine, ((0, 6), (0, 128 - seqs_here)))
    (scores_all,) = communicate("sequence_scores", 4, counts, gathers=[(mine, "dp", "vmem")])
    scores = jnp.transpose(scores_all[:, :2, :seqs_here], (1, 0, 2)).reshape(2, all_seqs)
    ratios = scores[1] - scores[0]
    chooser = (pairing[:, None] == jnp.arange(all_seqs)[None, :]).astype(f32)
    picked = jnp.sum(chooser * ratios[None, :], axis=1).reshape(-1, 2)
    margins = DPO_BETA * (picked[:, 0] - picked[:, 1])
    dpo_loss = jnp.sum(jax.nn.softplus(-margins))
    pair_pull = DPO_BETA * LOSS_SCALE * jax.nn.sigmoid(-margins)
    signed = jnp.stack([-pair_pull, pair_pull], axis=1).reshape(-1)
    coefficients = jnp.sum(signed[:, None] * chooser, axis=0)
    local_coef = lax.dynamic_slice_in_dim(coefficients, data_rank * seqs_here, seqs_here)
    token_coef = (local_coef[:, None] * living).reshape(tok_rows)
    grad_result = token_coef[:, None] * readout_wide
    post_dot = token_coef * stats[3]
    summed = shaped[1]
    scale_col = post_scale[1][:, None]
    result = hidden_wide + shaped * post_scale[:, :, None] * post_local
    grad_summed = (
        scale_col * post_local * grad_result
        - summed * scale_col**3 * post_dot[:, None] / full_width
    ).astype(bf16)
    (grad_wide,) = communicate("gather_grad", 5, counts, gathers=[(grad_summed, "tensor", "rows")])
    grad_mixed = dot(grad_wide, w_out_all).astype(bf16)
    grad_q_rot, rotated_key_gradient, value_head_gradient = attend_back(
        grad_mixed.reshape(seqs_here, length, q_heads, HEAD_SIZE),
        query_rows[seqs_here:],
        rotated_keys[seqs_here:],
        value_rows[seqs_here:],
        probs_low[seqs_here:],
        probabilities[seqs_here:],
        capped[seqs_here:],
    )
    query_rows_gradient = apply_rotation(grad_q_rot, -1.0).reshape(tok_rows, -1).astype(bf16)
    key_rows_gradient = (
        apply_rotation(rotated_key_gradient, -1.0).reshape(tok_rows, -1).astype(bf16)
    )
    value_rows_gradient = value_head_gradient.reshape(tok_rows, -1).astype(bf16)
    factor_terms = ADAPTER_SCALE * jnp.concatenate(
        [
            dot(low_rank_update[:, :rank_size], query_rows_gradient, rows_contraction),
            dot(low_rank_update[:, rank_size:], value_rows_gradient, rows_contraction),
        ],
        axis=1,
    )
    hook_terms = ADAPTER_SCALE * jnp.concatenate(
        [
            dot(query_rows_gradient, query_second_factor, contract_cols),
            dot(value_rows_gradient, value_second_factor, contract_cols),
        ],
        axis=1,
    )
    input_terms = (
        dot(query_rows_gradient, w_query_all, contract_cols)
        + dot(key_rows_gradient, w_key_all, contract_cols)
        + dot(value_rows_gradient, w_value_all, contract_cols)
    ).astype(bf16)
    hook_all, factor_all, grad_normed = communicate(
        "scatter_grad",
        6,
        counts,
        gathers=[
            (hook_terms.astype(bf16), "tensor", "vmem"),
            (factor_terms.astype(bf16), "dp", "vmem"),
        ],
        reduces=[input_terms],
    )
    factor_gradient = jnp.sum(factor_all.astype(f32), axis=0)
    query_factor_gradient = factor_gradient[:, : query_second_factor.shape[1]]
    value_factor_gradient = factor_gradient[:, query_second_factor.shape[1] :]
    hook = jnp.sum(hook_all.astype(f32), axis=0).astype(bf16)
    adapter_term = dot(pol_normed, hook, rows_contraction)
    slice_rows = full_width // (counts["dp"] * counts["tensor"])
    adapter_term = adapter_term.reshape(counts["dp"], counts["tensor"], slice_rows, -1)
    adapter_mine = lax.dynamic_index_in_dim(adapter_term, tensor_rank, 1, keepdims=False)
    a_local = lax.dynamic_slice_in_dim(a_both, tensor_rank * part_width, part_width)
    grad_normed = grad_normed + dot(hook, a_local, contract_cols)
    narrow = pol_hidden.astype(f32)
    pre_sums = jnp.sum(narrow * pre_local * grad_normed, axis=1)
    pre_sums = jnp.pad(pre_sums[None, :], ((0, 7), (0, 0)))
    adapter_blocks, pre_all = communicate(
        "adapter_parts",
        7,
        counts,
        gathers=[(adapter_mine.astype(bf16), "dp", "vmem"), (pre_sums, "tensor", "vmem")],
    )
    adapter_rows = jnp.sum(
        lax.dynamic_index_in_dim(adapter_blocks, data_rank, 1, keepdims=False).astype(f32), axis=0
    )
    (adapter_all,) = communicate(
        "adapter_gather", 8, counts, gathers=[(adapter_rows.astype(bf16), "tensor", "vmem")]
    )
    grad_a = adapter_all.reshape(-1, adapter_all.shape[-1]).astype(f32)
    pre_dot = jnp.sum(pre_all[:, 0, :], axis=0)
    grad_hidden = (
        grad_result
        + pol_scale * pre_local * grad_normed
        - narrow * pol_scale**3 * pre_dot[:, None] / full_width
    )
    return (
        result[1].astype(bf16),
        result[0].astype(bf16),
        dpo_loss,
        grad_hidden.astype(bf16),
        grad_a,
        query_factor_gradient,
        value_factor_gradient,
    )


def solution(mesh):
    placed = (
        P("dp", "tensor"),
        P("dp", "tensor"),
        P("dp", "tensor"),
        P("dp"),
        P(),
        P(),
        P(),
        P("dp", "tensor"),
        P("dp", "tensor"),
        P("dp", "tensor"),
        P("dp", "tensor"),
        P("dp", None),
        P("dp", None),
        P(None, "tensor"),
        P(None, "tensor"),
    )
    return jax.shard_map(
        body,
        mesh=mesh,
        in_specs=placed,
        out_specs=(
            P("dp", "tensor"),
            P("dp", "tensor"),
            P(),
            P("dp", "tensor"),
            P("dp", None),
            P(None, "tensor"),
            P(None, "tensor"),
        ),
        check_vma=False,
    )
```

profile of v0, /device:TPU:0, one launch (start us, length us, event | category | flops | bytes accessed | tf_op | source)
XLA Modules:
  0.0 409.3 jit_solution(5733994762332524770)
XLA Ops:
  4.4 1.3 reshape.314.refs_3_
  6.1 1.1 copy.83
  7.3 1.1 copy.84
  8.4 0.9 pad_maximum_fusion.1.refs_0_
  9.4 1.2 mul.555
  11.6 99.1 %gather_inputs.1 = (bf16[4,1152,128]{2,1,0:T(8,128)(2,1)}, bf16[4,1152,512]{2,1,0:T(8,128)(2,1)}, bf16[576,4608]{1,0:T(8,128)(2,1)}, f32[576,1]{1,0:T(8,128)}, b...) custom-call(bf16[1152,128]{1,0:T(8,128)(2,1)} %pad_maximum_fusion.1.refs_0_, ...), custom_call_target="tpu_custom_call" | custom-call | tf_op jit(solution)/shard_map/gather_inputs/pallas_call | solution.py:426
  110.7 1.1 slice_reduce_fusion
  111.8 3.1 fusion.20
  115.1 4.0 fusion.17
  119.6 6.3 %convolution_add_fusion.2 = f32[576,512]{1,0:T(8,128)S(1)} fusion(bf16[576,4608]{1,0:T(8,128)(2,1)} %get-tuple-element.19, bf16[4608,512]{1,0:T(8,128)(2,1)} %bitcast.129, f32[288,512]{1,0:T(8,128)S(1)} %convolution_multiply_fusion.1), kind=kOutput, calls=%fused_computation.20 | convolution fusion | flops 2718203904 | bytes 11796480 | tf_op jit(solution)/shard_map/dot_general | solution.py:470
  126.2 0.8 subtract_convert_fusion
  127.5 0.9 copy.86
  128.4 0.9 copy.87
  130.1 2.5 copy.85
  132.6 4.3 %fusion.116 = f32[6,96,2,128]{3,1,2,0:T(8,128)S(1)} fusion(bf16[6,96,4608,1]{2,1,3,0:T(8,128)(2,1)} %bitcast.139, bf16[2,128,4608,1]{2,1,0,3:T(8,128)(2,1)} %bitcast.134), kind=kOutput, calls=%fused_computation.185 | convolution fusion | flops 1358954496 | bytes 8257536 | tf_op jit(solution)/shard_map/dot_general | solution.py:470
  138.3 0.9 fusion.24
  139.2 1.4 fusion.113
  141.4 1.0 reshape_reshape.6
  142.4 1.9 slice_bitcast_fusion
  144.3 3.0 copy.102
  147.3 7.8 %convolution_convert_fusion.refs_0_ = bf16[576,4608]{1,0:T(8,128)(2,1)} fusion(bf16[576,512]{1,0:T(8,128)(2,1)} %reshape_reshape.6, bf16[4608,512]{1,0:T(8,128)(2,1)} %bitcast.148), kind=kOutput, calls=%fused_computation.1 | convolution fusion | flops 2720563200 | bytes 10616832 | tf_op jit(solution)/shard_map/dot_general | solution.py:470
  155.1 74.4 %scatter_out.1 = f32[576,576]{1,0:T(8,128)} custom-call(bf16[576,4608]{1,0:T(8,128)(2,1)} %convolution_convert_fusion.refs_0_), custom_call_target="tpu_custom_call" | custom-call | tf_op jit(solution)/shard_map/scatter_out/pallas_call | solution.py:426
  229.5 2.3 multiply_reduce_fusion.1
  232.6 10.0 %token_sums.1 = f32[8,8,288]{2,1,0:T(8,128)} custom-call(f32[8,288]{1,0:T(8,128)} %maximum_maximum_fusion.refs_0_), custom_call_target="tpu_custom_call" | custom-call | tf_op jit(solution)/shard_map/token_sums/pallas_call | solution.py:426
  242.6 0.9 reduce_sum.151
  243.9 0.9 slice_bitcast_fusion.1
  245.6 5.8 %sequence_scores.1 = f32[4,8,128]{2,1,0:T(8,128)} custom-call(f32[8,128]{1,0:T(8,128)} %pad.18.refs_0_), custom_call_target="tpu_custom_call" | custom-call | tf_op jit(solution)/shard_map/sequence_scores/pallas_call | solution.py:426
  253.8 1.0 subtract_convert_fusion.1.refs_0_
  254.8 46.4 %gather_grad.1 = bf16[288,4608]{1,0:T(8,128)(2,1)} custom-call(bf16[288,576]{1,0:T(8,128)(2,1)} %subtract_convert_fusion.1.refs_0_), custom_call_target="tpu_custom_call" | custom-call | tf_op jit(solution)/shard_map/gather_grad/pallas_call | solution.py:426
  301.3 5.4 %convolution_convert_fusion.2 = bf16[288,512]{1,0:T(8,128)(2,1)} fusion(bf16[288,4608]{1,0:T(8,128)(2,1)} %gather_grad.1, bf16[4608,512]{1,0:T(8,128)(2,1)} %bitcast.149), kind=kOutput, calls=%fused_computation.31 | convolution fusion | flops 1359101952 | bytes 7667712 | tf_op jit(solution)/shard_map/dot_general | solution.py:470
  306.7 1.1 reshape_reshape.7
  308.5 1.2 convolution_bitcast_fusion
  309.7 2.3 fusion.25
  312.0 2.2 convolution_bitcast_fusion.1
  315.0 0.8 multiply_subtract_fusion
  318.1 4.1 fusion.47
  322.2 0.9 convolution_add_fusion.1
  323.9 2.4 fusion.1.refs_2_
  326.3 47.6 %scatter_grad.1 = (bf16[8,288,128]{2,1,0:T(8,128)(2,1)}, bf16[4,64,768]{2,1,0:T(8,128)(2,1)}, f32[288,576]{1,0:T(8,128)}) custom-call(bf16[288,128]{1,0:T(8,128)(2,1)} %fusion.81.refs_0_, bf16[64,768]{1,0:T(8,128)(2,1)} %fusion.68.refs_1_, bf16[288,4608]{1,0:T(8,128)(2,1)} %fusion.1.refs_2_), custom_call_target="tpu_custom_call" | custom-call | tf_op jit(solution)/shard_map/scatter_grad/pallas_call | solution.py:426
  373.9 1.1 reduce_sum.157
  375.0 3.2 fusion.2
  378.2 1.4 fusion.35
  382.2 10.2 %adapter_parts.1 = (bf16[4,4,144,128]{3,2,1,0:T(8,128)(2,1)}, f32[8,8,288]{2,1,0:T(8,128)}) custom-call(bf16[4,144,128]{2,1,0:T(8,128)(2,1)} %fusion.73.refs_0_, f32[8,288]{1,0:T(8,128)} %pad.19.refs_1_), custom_call_target="tpu_custom_call" | custom-call | tf_op jit(solution)/shard_map/adapter_parts/pallas_call | solution.py:426
  392.4 0.9 slice_reduce_fusion.1
  393.3 1.1 fusion.33
  394.4 1.6 dynamic-slice_reduce_fusion.refs_0_
  396.0 11.5 %adapter_gather.1 = bf16[8,144,128]{2,1,0:T(8,128)(2,1)} custom-call(bf16[144,128]{1,0:T(8,128)(2,1)} %dynamic-slice_reduce_fusion.refs_0_), custom_call_target="tpu_custom_call" | custom-call | tf_op jit(solution)/shard_map/adapter_gather/pallas_call | solution.py:426
  407.5 1.8 bitcast_convert_fusion
  (125 shorter events, 20.9 us)
Async XLA Ops:
  0.6 118.7 %copy-start = (bf16[64,512]{1,0:T(8,128)(2,1)S(1)}, bf16[64,512]{1,0:T(8,128)(2,1)}, u32[]{:S(2)}) copy-start(bf16[64,512]{1,0:T(8,128)(2,1)} %param.28) | copy-start | bytes 196612
  0.6 8.6 %copy-start.6 = (bf16[288,576]{1,0:T(8,128)(2,1)S(1)}, bf16[288,576]{1,0:T(8,128)(2,1)}, u32[]{:S(2)}) copy-start(bf16[288,576]{1,0:T(8,128)(2,1)} %param.17) | copy-start | bytes 995332
  9.3 1.3 copy-start.19
  9.3 1.3 copy-start.8
  10.7 0.9 copy-start.4
  111.8 3.1 copy-start.22
  111.8 3.3 copy-start.9
  127.5 2.6 copy-start.2
  136.9 1.1 copy-start.16
  136.9 1.3 copy-start.17
  137.2 1.9 copy-start.20
  137.2 1.9 copy-start.21
  139.1 1.4 copy-start.13
  140.5 0.8 copy-start.11
  229.5 2.5 copy-start.25
  229.5 14.0 %copy-start.1 = (f32[576,576]{1,0:T(8,128)S(1)}, f32[576,576]{1,0:T(8,128)}, u32[]{:S(2)}) copy-start(f32[576,576]{1,0:T(8,128)} %scatter_out.1) | copy-start | bytes 3981316
  229.5 14.0 %copy-start.5 = (bf16[576,576]{1,0:T(8,128)(2,1)S(1)}, bf16[576,576]{1,0:T(8,128)(2,1)}, u32[]{:S(2)}) copy-start(bf16[576,576]{1,0:T(8,128)(2,1)} %copy-done.4) | copy-start | bytes 1990660
  243.9 8.4 %copy-start.26 = (s32[12]{0:T(128)S(1)}, s32[12]{0:T(128)}, u32[]{:S(2)}) copy-start(s32[12]{0:T(128)} %param.19) | copy-start | bytes 148
  243.9 9.8 %copy-start.24 = (s32[3]{0:T(128)S(1)}, s32[3]{0:T(128)}, u32[]{:S(2)}) copy-start(s32[3]{0:T(128)} %param.18) | copy-start | bytes 40
  243.9 9.9 %copy-start.7 = (bf16[288,576]{1,0:T(8,128)(2,1)S(1)}, bf16[288,576]{1,0:T(8,128)(2,1)}, u32[]{:S(2)}) copy-start(bf16[288,576]{1,0:T(8,128)(2,1)} %param.17) | copy-start | bytes 995332
  301.2 6.6 %copy-start.12 = (bf16[6,2,2,96,96]{3,4,2,1,0:T(8,128)(2,1)S(1)}, bf16[6,2,2,96,96]{3,4,2,1,0:T(8,128)(2,1)}, u32[]{:S(2)}) copy-start(bf16[6,2,2,96,96]{3,4,2,1,0:T(8,128)(2,1)} %copy-done.11) | copy-start | bytes 1327108
  306.7 3.0 copy-start.14
  312.0 2.7 copy-start.23
  318.1 4.1 copy-start.3
  322.2 1.7 copy-start.10
  375.0 3.2 copy-start.15
  378.2 2.7 copy-start.18
where the time goes:
time: 410 us; the launch traced here: 409 us
  Pallas kernels  305 us (74%)
  matrix products  51.2 us (12%)
  local copies, waits for them, and re-layouts  28.7 us (7%)
  other arithmetic  23.2 us (6%)
    pallas_call x8, Pallas kernels, communicate(): pl.pallas_call(kernel, name=name, out_shape=out_shapes, in_specs=in_specs...  305 us
    dot_general x17, matrix products, dot(): return lax.dot_general(a, b, dims, preferred_element_type=f32)  44.1 us

commit v1 on v0

v1 whole, which is shorter than its diff:
```python
import jax
import jax.numpy as jnp
import numpy as np
from jax import lax
from jax.experimental import pallas as pl
from jax.experimental.pallas import tpu as pltpu
from jax.sharding import PartitionSpec as P

MODEL_WIDTH = 4608
HQ = 32
HEAD_SIZE = 128


NORM_EPS = 1e-06
SOFT_CAP = 50.0
ADAPTER_SCALE = 0.5
DPO_BETA = 0.5
LOSS_SCALE = 256.0
ROPE_BASE = 10000.0

MESH = pl.DeviceIdType.MESH
VMEM_GRANT = 67_000_000
LANES = 128
f32, bf16 = jnp.float32, jnp.bfloat16
NT = (((1,), (1,)), ((), ()))
TN = (((0,), (0,)), ((), ()))


def query_scale():
    return float(MODEL_WIDTH // HQ) ** (-0.5)


def grid_of(axis, count):
    if axis == "dp":
        inner = 2 if count % 2 == 0 else 1
    else:
        inner = 1
        while (inner * 2) ** 2 <= count and count % (inner * 2) == 0:
            inner *= 2
    return count // inner, inner


def pick(size, options):
    for option in options:
        if size % option == 0:
            return option
    return size


def rope_tables(length):
    half = HEAD_SIZE // 2
    spacing = ROPE_BASE ** (-2.0 * np.arange(half, dtype=np.float32) / HEAD_SIZE)
    angles = np.arange(length, dtype=np.float32)[:, None] * spacing[None, :].astype(np.float32)
    cosine, sine = np.cos(angles), np.sin(angles)
    return (
        np.concatenate([cosine, cosine], axis=1).astype(np.float32),
        np.concatenate([-sine, sine], axis=1).astype(np.float32),
    )


def dot(x, y, dims=(((1,), (0,)), ((), ()))):
    return lax.dot_general(x, y, dims, preferred_element_type=f32)


def remote(src, dst, send_sem, recv_sem, axis, rank):
    return pltpu.make_async_remote_copy(
        src_ref=src,
        dst_ref=dst,
        send_sem=send_sem,
        recv_sem=recv_sem,
        device_id={axis: rank},
        device_id_type=MESH,
    )


class Sizes:
    def __init__(self, tok_rows, part_width, seqs, dp, tensor, q_cols, k_cols, rank):
        self.R, self.PW, self.S, self.D, self.T = tok_rows, part_width, seqs, dp, tensor
        self.L = tok_rows // seqs
        self.QC, self.KC = q_cols, k_cols
        self.AR = 2 * rank
        self.rank = rank
        self.NC = q_cols + 2 * k_cols
        self.NW = self.NC + self.AR
        self.O, self.I = grid_of("tensor", tensor)
        self.Y, self.C = grid_of("dp", dp)
        self.r = tensor // dp
        self.gp = max(self.O // self.Y, 1)
        self.KV = k_cols // HEAD_SIZE
        self.G = q_cols // k_cols
        self.P = self.L
        self.n = tok_rows // self.P
        self.Rp = -(-tok_rows // LANES) * LANES
        self.W = part_width * tensor
        self.step = pick(tok_rows, (48, 32, 16))
        size = 16
        while tok_rows % size or tok_rows // size > tensor:
            size += 16
        self.HR, self.HN = size, tok_rows // size


def vm(*shape, kind=bf16):
    return pltpu.VMEM(shape, kind)


def sem(*counts):
    return [pltpu.SemaphoreType.DMA((max(count, 1),)) for count in counts]


def build_scratch(z):
    R, PW, T, D, O, I, n = z.R, z.PW, z.T, z.D, z.O, z.I, z.n
    inner = O * (I - 1)
    moved = z.QC + z.KC

    def boxes():
        return [vm(T, R, PW), vm(max(inner, 1), R, PW), vm(O, R, PW), vm(O, R, PW)]

    def reduce_sems():
        return sem(inner * n, inner * n, O * n, O * n, O * n)

    def gather_sems(count):
        return sem(T * count, O * count, O * count, inner * count)

    def stat():
        return [vm(T, 8, z.Rp, kind=f32), vm(8, z.Rp, kind=f32)] + sem(T, T)

    def weight_sems():
        return sem(D * z.r, (z.Y - 1) * z.r, z.Y * (z.C - 1) * z.r)

    return dict(
        held=vm(T, 2 * R, PW),
        normed=vm(T, 2 * R, PW),
        W=vm(D, z.r * PW, z.NW),
        WO=vm(D, z.r * PW, z.QC),
        acc=vm(2 * R, z.NW, kind=f32),
        added=vm(R, moved, kind=f32),
        low=vm(R, z.AR),
        F=vm(z.AR, moved),
        q2=vm(z.S, z.KV, z.G * z.L, HEAD_SIZE),
        kk=vm(z.S, z.KV, z.L, HEAD_SIZE),
        vv=vm(z.S, z.KV, z.L, HEAD_SIZE),
        probs=vm(z.S, z.KV, z.G * z.L, z.L, kind=f32),
        capped=vm(z.S, z.KV, z.G * z.L, z.L, kind=f32),
        mixed=vm(2 * R, z.QC),
        pol=boxes(),
        ref=boxes(),
        pol_sems=reduce_sems(),
        ref_sems=reduce_sems(),
        grad_sems=reduce_sems(),
        piece=vm(z.P, PW, kind=f32),
        summed=vm(2 * R, PW, kind=f32),
        gheld=vm(T, R, PW),
        gm=vm(R, z.QC, kind=f32),
        gmb=vm(R, z.QC),
        dcat=vm(R, z.NW),
        gnorm=vm(R, PW, kind=f32),
        col=vm(2 * R, 1, kind=f32),
        scol=vm(2 * R, 1, kind=f32),
        liv=vm(R, 1, kind=f32),
        ccol=vm(R, 1, kind=f32),
        pcol=vm(4 * R, 1, kind=f32),
        s0=stat(),
        s1=stat(),
        s2=stat(),
        s3=stat(),
        score=[vm(D, 8, LANES, kind=f32), vm(8, LANES, kind=f32)] + sem(D, D),
        hbox=vm(T, z.HR, z.AR),
        hsum=vm(z.HN, z.HR, z.AR),
        h1=sem(T, T),
        h2=sem(T, T),
        fac=[vm(D, z.rank, moved), vm(z.rank, moved)] + sem(D, D),
        ad=[vm(D, z.r * PW, z.AR), vm(D, z.r * PW, z.AR)] + sem(D, D),
        load=sem(8),
        hid=[gather_sems(n), gather_sems(n)],
        gag=gather_sems(n),
        wq=weight_sems(),
        wo=weight_sems(),
    )


class Refs:
    pass


class Gather:
    def __init__(self, z, place, held, sems, row=0):
        self.z, self.place, self.held, self.pieces = z, place, held, z.n
        self.r, self.u, self.d, self.x = sems
        self.row = row

    def block(self, slot, c):
        return self.held.at[slot, pl.ds(self.row + c * self.z.P, self.z.P)]

    def copy(self, aa, c, kind, k=0):
        z, (a, b) = self.z, self.place
        slot = aa * z.I + b
        block = self.block(slot, c)
        at = aa * self.pieces + c
        if kind == "up":
            send, rank = self.u.at[at], lax.rem(a + 1, z.O) * z.I + b
        elif kind == "dn":
            send, rank = self.d.at[at], lax.rem(a + z.O - 1, z.O) * z.I + b
        else:
            send = self.x.at[(aa * (z.I - 1) + k - 1) * self.pieces + c]
            rank = a * z.I + lax.rem(b + k, z.I)
        return remote(block, block, send, self.r.at[slot * self.pieces + c], "tensor", rank)

    def wait_recv(self, slot, c):
        z = self.z
        block = self.block(slot, c)
        at = slot * self.pieces + c
        remote(block, block, self.u.at[0], self.r.at[at], "tensor", 0).wait_recv()

    def sends(self, aa, c, act):
        z, (a, b) = self.z, self.place

        @pl.when((aa <= a) & (a < z.O - 1))
        def _():
            act(self.copy(aa, c, "up"))

        @pl.when((aa >= a) & (a > 0))
        def _():
            act(self.copy(aa, c, "dn"))

        for k in range(1, z.I):
            act(self.copy(aa, c, "x", k))

    def start(self):
        for c in range(self.pieces):
            self.sends(self.place[0], c, lambda copy: copy.start())

    def relay(self, aa):
        z, (a, b) = self.z, self.place

        @pl.loop(0, self.pieces)
        def _(c):
            self.wait_recv(aa * z.I + b, c)
            self.sends(aa, c, lambda copy: copy.start())

    def wait_inner(self, aa):
        z, (a, b) = self.z, self.place
        for k in range(1, z.I):

            @pl.loop(0, self.pieces)
            def _(c, k=k):
                self.wait_recv(aa * z.I + lax.rem(b + k, z.I), c)

    def drain(self):
        @pl.loop(0, self.z.O)
        def _(aa):
            @pl.loop(0, self.pieces)
            def _(c):
                self.sends(aa, c, lambda copy: copy.wait_send())


class Reduce:
    def __init__(self, z, place, bufs, sems, piece, out, out_row):
        self.z, self.place, self.piece = z, place, piece
        self.stage, self.near, self.up, self.dn = bufs
        self.sx, self.rx, self.sz, self.ru, self.rd = sems
        self.out, self.out_row = out, out_row

    def rows(self, c):
        return pl.ds(c * self.z.P, self.z.P)

    def x_copy(self, aa, k, c):
        z, (a, b) = self.z, self.place
        at = aa * (z.I - 1) + k - 1
        return remote(
            self.stage.at[aa * z.I + lax.rem(b + k, z.I), self.rows(c)],
            self.near.at[at, self.rows(c)],
            self.sx.at[at * z.n + c],
            self.rx.at[at * z.n + c],
            "tensor",
            a * z.I + lax.rem(b + k, z.I),
        )

    def z_copy(self, aa, c, up):
        z, (a, b) = self.z, self.place
        box, sem = (self.up, self.ru) if up else (self.dn, self.rd)
        rank = lax.rem(a + (1 if up else z.O - 1), z.O) * z.I + b
        at = aa * z.n + c
        return remote(
            self.stage.at[aa * z.I + b, self.rows(c)],
            box.at[aa, self.rows(c)],
            self.sz.at[at],
            sem.at[at],
            "tensor",
            rank,
        )

    def produce(self, aa, k, term):
        z, (a, b) = self.z, self.place
        slot = aa * z.I + lax.rem(b + k, z.I)
        self.stage[slot] = term(slot).astype(bf16)
        if k:
            for c in range(z.n):
                self.x_copy(aa, k, c).start()

    def collect(self, aa):
        z, (a, b) = self.z, self.place

        @pl.loop(0, z.n)
        def _(c):
            rows = pl.ds(pl.multiple_of(c * z.P, 16), z.P)
            value = self.stage[aa * z.I + b, rows, :].astype(f32)
            for k in range(1, z.I):
                self.x_copy(aa, k, c).wait_recv()
                value += self.near[aa * (z.I - 1) + k - 1, rows, :].astype(f32)
            self.piece[...] = value

            @pl.when((aa >= a) & (a > 0))
            def _():
                self.z_copy(aa, c, True).wait_recv()
                self.piece[...] += self.up[aa, rows, :].astype(f32)

            @pl.when((aa <= a) & (a < z.O - 1))
            def _():
                self.z_copy(aa, c, False).wait_recv()
                self.piece[...] += self.dn[aa, rows, :].astype(f32)

            @pl.when(aa == a)
            def _():
                at = pl.ds(pl.multiple_of(self.out_row + c * z.P, 8), z.P)
                self.out[at, :] = self.piece[...]

            @pl.when(aa != a)
            def _():
                self.stage[aa * z.I + b, rows, :] = self.piece[...].astype(bf16)

            @pl.when(aa > a)
            def _():
                self.z_copy(aa, c, True).start()

            @pl.when(aa < a)
            def _():
                self.z_copy(aa, c, False).start()

    def drain(self):
        z, (a, b) = self.z, self.place

        @pl.loop(0, z.O)
        def _(aa):
            @pl.loop(0, z.n)
            def _(c):
                for k in range(1, z.I):
                    self.x_copy(aa, k, c).wait_send()

                @pl.when(aa != a)
                def _():
                    self.z_copy(aa, c, True).wait_send()


class Exchange:
    def __init__(self, axis, rank, count, box, own, send, recv):
        self.axis, self.rank, self.count, self.box, self.own = axis, rank, count, box, own
        self.send, self.recv = send, recv

    def copy(self, k):
        peer = lax.rem(self.rank + k, self.count)
        own = self.own.at[peer] if len(self.own.shape) == len(self.box.shape) else self.own
        return remote(
            own, self.box.at[self.rank], self.send.at[k], self.recv.at[self.rank], self.axis, peer
        )

    def start(self):
        for k in range(1, self.count):
            self.copy(k).start()

    def wait(self):
        for k in range(1, self.count):
            peer = lax.rem(self.rank + k, self.count)
            slot = self.box.at[peer]
            remote(slot, slot, self.send.at[k], self.recv.at[peer], self.axis, peer).wait_recv()

    def total(self):
        value = self.box[0].astype(f32)
        for k in range(1, self.count):
            value += self.box[k].astype(f32)
        return value

    def drain(self):
        for k in range(1, self.count):
            self.copy(k).wait_send()


def rope(x, cosine, sine):
    return x * cosine + pltpu.roll(x, HEAD_SIZE // 2, 1) * sine


def make_kernel(z, names, scratch):
    R, PW, T, D, O, I, C, Y = z.R, z.PW, z.T, z.D, z.O, z.I, z.C, z.Y
    L, S, QC, KC, NC, NW = z.L, z.S, z.QC, z.KC, z.NC, z.NW
    n_tile = pick(NW, (384, 512, 256, 128))

    def kernel(*refs):
        m = Refs()
        work = jax.tree.unflatten(jax.tree.structure(scratch), refs[len(names) :])
        for name, ref in [*zip(names, refs), *work.items()]:
            setattr(m, name, ref)
        t, d = lax.axis_index("tensor"), lax.axis_index("dp")
        a, b = lax.div(t, I), lax.rem(t, I)
        y, core = lax.div(d, C), lax.rem(d, C)
        place = (a, b)
        lane = lax.broadcasted_iota(jnp.int32, (1, LANES), 1)

        held, normed, W, WO, acc = m.held, m.normed, m.W, m.WO, m.acc

        def to_lanes(column):
            eye = lax.broadcasted_iota(jnp.int32, (R, z.Rp), 0) == lax.broadcasted_iota(
                jnp.int32, (R, z.Rp), 1
            )
            return jnp.sum(jnp.where(eye, column, 0.0), axis=0, keepdims=True)

        def to_column(row):
            eye = lax.broadcasted_iota(jnp.int32, (R, z.Rp), 0) == lax.broadcasted_iota(
                jnp.int32, (R, z.Rp), 1
            )
            return jnp.sum(jnp.where(eye, row, 0.0), axis=1, keepdims=True)

        def stack_rows(rows):
            index = lax.broadcasted_iota(jnp.int32, (8, z.Rp), 0)
            out = jnp.zeros((8, z.Rp), f32)
            for i, row in enumerate(rows):
                out = jnp.where(index == i, row, out)
            return out

        def chunks(fn, total=R):
            @pl.loop(0, total // z.step)
            def _(i):
                fn(pl.ds(pl.multiple_of(i * z.step, 16), z.step))

        def exchange(refs, count=T, axis="tensor", rank=t):
            return Exchange(axis, rank, count, *refs)

        loads = [
            (m.pol_hidden, held.at[t, pl.ds(0, R)]),
            (m.ref_hidden, held.at[t, pl.ds(R, R)]),
            (m.w_query, W.at[d, :, pl.ds(0, QC)]),
            (m.w_key, W.at[d, :, pl.ds(QC, KC)]),
            (m.value_projection, W.at[d, :, pl.ds(QC + KC, KC)]),
            (m.a_both, W.at[d, :, pl.ds(NC, z.AR)]),
            (m.w_out, WO.at[d]),
        ]
        copies = [
            pltpu.make_async_copy(src, dst, m.load[0].at[i]) for i, (src, dst) in enumerate(loads)
        ]
        for copy in copies:
            copy.start()

        barrier = pltpu.get_barrier_semaphore()
        for k in range(1, T):
            pl.semaphore_signal(
                barrier, inc=1, device_id={"tensor": lax.rem(t + k, T)}, device_id_type=MESH
            )
        for k in range(1, D):
            pl.semaphore_signal(
                barrier, inc=1, device_id={"dp": lax.rem(d + k, D)}, device_id_type=MESH
            )

        acc[...] = jnp.zeros_like(acc)
        m.F[...] = jnp.zeros_like(m.F)
        m.F[0 : z.rank, 0:QC] = m.query_second_factor[...]
        m.F[z.rank :, QC:] = m.value_second_factor[...]
        for s in range(S):
            slot = lax.broadcasted_iota(jnp.int32, (L, 1), 0)
            m.liv[s * L : (s + 1) * L, :] = (slot < m.lengths[s]).astype(f32)

        def square(rows):
            x = held[t, rows, :].astype(f32)
            m.col[rows, :] = jnp.sum(x * x, axis=1, keepdims=True)

        stats0 = exchange(m.s0)
        copies[0].wait()
        copies[1].wait()
        chunks(square, 2 * R)
        stats0.own[...] = stack_rows([to_lanes(m.col[0:R]), to_lanes(m.col[R:])])
        stats0.box[t] = stats0.own[...]
        pl.semaphore_wait(barrier, T - 1 + D - 1)
        stats0.start()

        hid = [Gather(z, place, held, m.hid[model], model * R) for model in range(2)]
        hid[0].start()
        hid[1].start()

        def weight_copy(job, slot, piece, k, far):
            buf, (recv, across, beside) = job
            block = buf.at[slot, pl.ds(piece * PW, PW)]
            if far:
                send = across.at[(k - 1) * z.r + piece]
                rank = lax.rem(y + k, Y) * C + core
            else:
                send = beside.at[(lax.div(slot, C) * (C - 1) + k - 1) * z.r + piece]
                rank = y * C + lax.rem(core + k, C)
            return remote(block, block, send, recv.at[slot * z.r + piece], "dp", rank)

        def order_of(q):
            return lax.rem(b + 1 + q, z.r)

        def weights_start(job):
            for q in range(z.r):
                for k in range(1, Y):
                    weight_copy(job, d, order_of(q), k, True).start()
                for k in range(1, C):
                    weight_copy(job, d, order_of(q), k, False).start()

        def weights_wait(job, slot, piece):
            weight_copy(job, slot, piece, 1, Y > 1).wait_recv()

        def weights_relay(job, q):
            for jj in range(1, Y):
                slot = lax.rem(y + jj, Y) * C + core
                weights_wait(job, slot, order_of(q))
                for k in range(1, C):
                    weight_copy(job, slot, order_of(q), k, False).start()

        def weights_wait_core(job, yy, q):
            for k in range(1, C):
                weights_wait(job, yy * C + lax.rem(core + k, C), order_of(q))

        def weights_drain(job):
            for q in range(z.r):
                for k in range(1, Y):
                    weight_copy(job, d, order_of(q), k, True).wait_send()
                for yy in range(Y):
                    for k in range(1, C):
                        weight_copy(job, yy * C + core, order_of(q), k, False).wait_send()

        wq, wo = (W, m.wq), (WO, m.wo)
        for copy in copies[2:6]:
            copy.wait()
        weights_start(wq)
        copies[6].wait()
        weights_start(wo)

        stats0.wait()

        scale = lax.rsqrt(stats0.total() / z.W + NORM_EPS)
        m.scol[0:R, :] = to_column(scale[0:1])
        m.scol[R:, :] = to_column(scale[1:2])

        def normalise(model, slot):
            gain = m.gains[pl.ds(slot, 1), :]

            def one(rows):
                at = pl.ds(pl.multiple_of(model * R + rows.start, 16), rows.size)
                x = held[slot, at, :].astype(f32)
                normed[slot, at, :] = (x * m.scol[at, :] * gain).astype(bf16)

            chunks(one)

        def arrive(model, aa):
            hid[model].wait_inner(aa)

            @pl.loop(0, I)
            def _(bb):
                normalise(model, aa * I + bb)

        def project(model, slot):
            row, count = model * R, R
            ws, off = lax.div(slot, z.r), lax.rem(slot, z.r) * PW

            @pl.loop(0, NW // n_tile)
            def _(i):
                cols = pl.ds(pl.multiple_of(i * n_tile, LANES), n_tile)
                acc[row : row + count, cols] += dot(
                    normed[slot, row : row + count, :],
                    W[ws, pl.ds(pl.multiple_of(off, 16), PW), cols],
                )

        def project_group(model, aa, stages):
            @pl.loop(0, I)
            def _(bb):
                slot = aa * I + bb
                near = lax.div(lax.div(slot, z.r), C) == y
                first = lax.rem(slot, z.r) != order_of(z.r - 1)
                kinds = [
                    near,
                    jnp.logical_not(near) & first,
                    jnp.logical_not(near) & jnp.logical_not(first),
                ]
                wanted = kinds[stages[0]]
                for stage in stages[1:]:
                    wanted = wanted | kinds[stage]

                @pl.when(wanted)
                def _():
                    project(model, slot)

        side = jnp.minimum(a, O - 1 - a)

        def visit(j):
            inside = jnp.where(lax.rem(j, 2) == 1, a - lax.div(j + 1, 2), a + lax.div(j, 2))
            outside = jnp.where(a <= O - 1 - a, a + j - side, a - j + side)
            return jnp.where(j <= 2 * side, inside, outside)

        for q in range(z.r):
            weights_wait_core(wq, y, q)

        @pl.loop(1, O)
        def _(j):
            hid[0].relay(visit(j))
            arrive(0, visit(j - 1))
            project_group(0, visit(j - 1), [0])

        for q in range(z.r - 1):
            weights_relay(wq, q)
            for jj in range(1, Y):
                weights_wait_core(wq, lax.rem(y + jj, Y), q)

        @pl.loop(1, O)
        def _(j):
            hid[1].relay(visit(j))

        arrive(0, visit(O - 1))
        project_group(0, visit(O - 1), [0])

        @pl.loop(0, O)
        def _(j):
            project_group(0, j, [1])

        @pl.loop(0, O - 1)
        def _(j):
            arrive(1, visit(j))
            project_group(1, visit(j), [0, 1])

        weights_relay(wq, z.r - 1)
        for jj in range(1, Y):
            weights_wait_core(wq, lax.rem(y + jj, Y), z.r - 1)

        @pl.loop(0, O)
        def _(j):
            project_group(0, j, [2])

        row_slot = lax.broadcasted_iota(jnp.int32, (L, L), 0)
        key_slot = lax.broadcasted_iota(jnp.int32, (L, L), 1)
        causal = key_slot <= row_slot

        def attend(model):
            base = model * R
            if model == 0:
                m.low[...] = acc[0:R, NC:NW].astype(bf16)
                m.added[...] = ADAPTER_SCALE * dot(m.low[...], m.F[...])

            @pl.loop(0, S)
            def _(s):
                rows = pl.ds(pl.multiple_of(base + s * L, 16), L)
                local = pl.ds(pl.multiple_of(s * L, 16), L)
                allowed = causal & (key_slot < m.lengths[s])
                allowed = jnp.concatenate([allowed.astype(f32)] * z.G, axis=0) > 0.5
                cosine, sine = m.cosine[...], m.sine[...]
                for k in range(z.KV):
                    head = slice(k * HEAD_SIZE, (k + 1) * HEAD_SIZE)
                    kh = acc[rows, QC + k * HEAD_SIZE : QC + (k + 1) * HEAD_SIZE]
                    vh = acc[rows, QC + KC + k * HEAD_SIZE : QC + KC + (k + 1) * HEAD_SIZE]
                    if model == 0:
                        vh = vh + m.added[local, QC + k * HEAD_SIZE : QC + (k + 1) * HEAD_SIZE]
                    kh = rope(kh, cosine, sine).astype(bf16)
                    vh = vh.astype(bf16)
                    queries = []
                    for g in range(z.G):
                        h = k * z.G + g
                        qh = acc[rows, h * HEAD_SIZE : (h + 1) * HEAD_SIZE]
                        if model == 0:
                            qh = qh + m.added[local, h * HEAD_SIZE : (h + 1) * HEAD_SIZE]
                        queries.append(rope(qh, cosine, sine).astype(bf16))
                    q2 = jnp.concatenate(queries, axis=0)
                    scores = dot(q2, kh, NT) * query_scale()
                    capped = SOFT_CAP * jnp.tanh(scores / SOFT_CAP)
                    weights = jnp.where(allowed, jnp.exp(capped), 0.0)
                    probs = weights / jnp.sum(weights, axis=1, keepdims=True)
                    out = dot(probs.astype(bf16), vh).astype(bf16)
                    for g in range(z.G):
                        h = k * z.G + g
                        m.mixed[rows, h * HEAD_SIZE : (h + 1) * HEAD_SIZE] = out[
                            g * L : (g + 1) * L
                        ]
                    if model == 0:
                        m.q2[s, k] = q2
                        m.kk[s, k] = kh
                        m.vv[s, k] = vh
                        m.probs[s, k] = probs
                        m.capped[s, k] = capped

        attend(0)

        def out_term(model):
            def term(slot):
                ws, off = lax.div(slot, z.r), lax.rem(slot, z.r) * PW
                return dot(
                    m.mixed[model * R : (model + 1) * R, :],
                    WO[ws, pl.ds(pl.multiple_of(off, 16), PW), :],
                    NT,
                )

            return term

        def reduce_of(bufs, sems, out, row):
            return Reduce(
                z,
                place,
                bufs,
                sems,
                m.piece,
                out,
                row,
            )

        red_pol = reduce_of(m.pol, m.pol_sems, m.summed, 0)
        red_ref = reduce_of(m.ref, m.ref_sems, m.summed, R)
        red_grad = reduce_of(m.pol, m.grad_sems, m.gnorm, 0)

        def near_first(j):
            yy, jj = lax.rem(y + lax.div(j, z.gp), Y), lax.rem(j, z.gp)
            low = yy * z.gp + jj
            high = yy * z.gp + z.gp - 1 - jj
            return jnp.where(2 * yy < Y, low, high)

        def far_first(j):
            return visit(O - 1 - j)

        def produce_range(red, first, last, order, term, ks):
            @pl.loop(first, last)
            def _(j):
                for k in ks:
                    red.produce(order(j), k, term)

        def collect_range(red, first, last, order):
            @pl.loop(first, last)
            def _(j):
                @pl.when(order(j) != a)
                def _():
                    red.collect(order(j))

        xs, own = list(range(1, I)), [0]
        for q in range(z.r):
            weights_wait_core(wo, y, q)
        produce_range(red_pol, 0, z.gp, near_first, out_term(0), xs + own)

        arrive(1, visit(O - 1))
        project_group(1, visit(O - 1), [0, 1])

        @pl.loop(0, O)
        def _(j):
            project_group(1, j, [2])

        attend(1)
        collect_range(red_pol, 0, z.gp, near_first)
        early = z.r if I != z.r else z.r - 1
        for q in range(early):
            weights_relay(wo, q)
            for jj in range(1, Y):
                weights_wait_core(wo, lax.rem(y + jj, Y), q)
        produce_range(red_pol, z.gp, O, near_first, out_term(0), xs)
        for q in range(early, z.r):
            weights_relay(wo, q)
            for jj in range(1, Y):
                weights_wait_core(wo, lax.rem(y + jj, Y), q)
        produce_range(red_pol, z.gp, O, near_first, out_term(0), own)
        produce_range(red_ref, 0, 1, far_first, out_term(1), xs + own)
        collect_range(red_pol, z.gp, O, near_first)
        produce_range(red_ref, 1, 2, far_first, out_term(1), xs + own)
        red_pol.collect(a)

        post_gain = m.gains[pl.ds(T + t, 1), :]

        def token_sums(model, refs):
            base = model * R

            def one(rows):
                at = pl.ds(base + rows.start, rows.size)
                x = m.summed[at, :]
                read = m.readout[rows, :].astype(f32)
                m.pcol[pl.ds(rows.start, rows.size), :] = jnp.sum(x * x, axis=1, keepdims=True)
                m.pcol[pl.ds(R + rows.start, rows.size), :] = jnp.sum(
                    x * (post_gain * read), axis=1, keepdims=True
                )
                h = held[t, at, :].astype(f32)
                m.pcol[pl.ds(2 * R + rows.start, rows.size), :] = jnp.sum(
                    h * read, axis=1, keepdims=True
                )

            chunks(one)
            done = exchange(refs)
            done.own[...] = stack_rows([to_lanes(m.pcol[i * R : (i + 1) * R]) for i in range(3)])
            done.box[t] = done.own[...]
            done.start()
            return done

        stats1 = token_sums(0, m.s1)
        produce_range(red_ref, 2, O, far_first, out_term(1), xs + own)
        stats1.wait()
        sums1 = stats1.total()
        post1 = lax.rsqrt(sums1[0:1] / z.W + NORM_EPS)
        m.col[0:R, :] = to_column(post1)
        m.col[R:, :] = to_column(post1 * post1 * post1 * sums1[1:2] / z.W)

        def make_grad(rows):
            read = m.readout[rows, :].astype(f32)
            value = m.col[rows, :] * post_gain * read - m.summed[rows, :] * m.col[
                pl.ds(R + rows.start, rows.size), :
            ]
            m.gheld[t, rows, :] = (value * m.liv[rows, :]).astype(bf16)

        chunks(make_grad)
        gag = Gather(z, place, m.gheld, m.gag)
        gag.start()

        def finish(model, out):
            def one(rows):
                at = pl.ds(model * R + rows.start, rows.size)
                h = held[t, at, :].astype(f32)
                out[rows, :] = (h + m.summed[at, :] * m.pcol[rows, :] * post_gain).astype(
                    bf16
                )

            chunks(one)

        m.pcol[0:R, :] = m.col[0:R, :]
        finish(0, m.policy_out)
        m.gm[...] = jnp.zeros_like(m.gm)

        def back_out(aa):
            @pl.loop(0, I)
            def _(bb):
                slot = aa * I + bb
                ws, off = lax.div(slot, z.r), lax.rem(slot, z.r) * PW
                m.gm[...] += dot(
                    m.gheld[slot], WO[ws, pl.ds(pl.multiple_of(off, 16), PW), :]
                )

        collect_range(red_ref, 0, O - 1, far_first)

        @pl.loop(1, O)
        def _(j):
            gag.relay(visit(j))

            @pl.when(j == O - 1)
            def _():
                red_ref.collect(a)

            gag.wait_inner(visit(j - 1))
            back_out(visit(j - 1))

        stats2 = token_sums(1, m.s2)
        gag.wait_inner(visit(O - 1))
        back_out(visit(O - 1))
        stats2.wait()
        sums2 = stats2.total()
        post2 = lax.rsqrt(sums2[0:1] / z.W + NORM_EPS)

        token_pol = sums1[2:3] + post1 * sums1[1:2]
        token_ref = sums2[2:3] + post2 * sums2[1:2]
        wide = lax.broadcasted_iota(jnp.int32, (1, z.Rp), 1)
        mine = jnp.zeros((1, LANES), f32)
        for s in range(S):
            inside = (wide >= s * L) & (wide < s * L + m.lengths[s])
            value = jnp.sum(jnp.where(inside, token_pol, 0.0), axis=1, keepdims=True) - jnp.sum(
                jnp.where(inside, token_ref, 0.0), axis=1, keepdims=True
            )
            mine = jnp.where(lane == d * S + s, value, mine)
        scores = exchange(m.score, D, "dp", d)
        scores.own[...] = jnp.broadcast_to(mine, (8, LANES))
        scores.box[d] = scores.own[...]
        scores.start()
        m.gmb[...] = m.gm[...].astype(bf16)

        @pl.loop(0, S)
        def _(s):
            rows = pl.ds(pl.multiple_of(s * L, 16), L)
            cosine, sine = m.cosine[...], -m.sine[...]
            for k in range(z.KV):
                parts = []
                for g in range(z.G):
                    h = k * z.G + g
                    parts.append(m.gmb[rows, h * HEAD_SIZE : (h + 1) * HEAD_SIZE])
                grad = jnp.concatenate(parts, axis=0)
                probs, capped = m.probs[s, k], m.capped[s, k]
                grad_probs = dot(grad, m.vv[s, k], NT)
                grad_v = dot(probs.astype(bf16), grad, TN)
                centered = grad_probs - jnp.sum(grad_probs * probs, axis=1, keepdims=True)
                ratio = capped / SOFT_CAP
                grad_scores = (
                    probs * centered * (1.0 - ratio * ratio) * query_scale()
                ).astype(bf16)
                grad_q = dot(grad_scores, m.kk[s, k])
                grad_k = dot(grad_scores, m.q2[s, k], TN)
                for g in range(z.G):
                    h = k * z.G + g
                    m.dcat[rows, h * HEAD_SIZE : (h + 1) * HEAD_SIZE] = rope(
                        grad_q[g * L : (g + 1) * L], cosine, sine
                    ).astype(bf16)
                at = QC + k * HEAD_SIZE
                m.dcat[rows, at : at + HEAD_SIZE] = rope(grad_k, cosine, sine).astype(bf16)
                m.dcat[rows, at + KC : at + KC + HEAD_SIZE] = grad_v.astype(bf16)

        m.dcat[:, NC:NW] = (
            ADAPTER_SCALE
            * (
                dot(m.dcat[:, 0:QC], m.F[:, 0:QC], NT)
                + dot(m.dcat[:, QC + KC : NC], m.F[:, QC:], NT)
            )
        ).astype(bf16)

        def in_term(slot):
            ws, off = lax.div(slot, z.r), lax.rem(slot, z.r) * PW
            return dot(m.dcat[...], W[ws, pl.ds(pl.multiple_of(off, 16), PW), :], NT)

        def pre_dot(rows):
            m.pcol[pl.ds(3 * R + rows.start, rows.size), :] = jnp.sum(
                m.dcat[rows, :].astype(f32) * acc[rows, :], axis=1, keepdims=True
            )

        def hook_part(part, k):
            return remote(
                m.dcat.at[pl.ds(pl.multiple_of(part * z.HR, 16), z.HR), pl.ds(NC, z.AR)],
                m.hbox.at[t],
                m.h1[0].at[k],
                m.h1[1].at[t],
                "tensor",
                lax.rem(t + k, T),
            )

        def hook_whole(k):
            mine = m.hsum.at[t]
            peer = lax.rem(t + k, T)
            return remote(mine, mine, m.h2[0].at[k], m.h2[1].at[t], "tensor", peer)

        for k in range(1, T):
            peer = lax.rem(t + k, T)

            @pl.when(peer < z.HN)
            def _(peer=peer, k=k):
                hook_part(peer, k).start()

        chunks(pre_dot)
        stats3 = exchange(m.s3)
        stats3.own[...] = stack_rows([to_lanes(m.pcol[3 * R :])])
        stats3.box[t] = stats3.own[...]
        stats3.start()
        red_pol.drain()
        produce_range(red_grad, 0, 1, far_first, in_term, xs + own)

        @pl.when(t < z.HN)
        def _():
            at = pl.ds(pl.multiple_of(t * z.HR, 16), z.HR)
            m.hbox[t] = m.dcat[at, NC:NW]
            for k in range(1, T):
                peer = lax.rem(t + k, T)
                slot = m.hbox.at[peer]
                remote(slot, slot, m.h1[0].at[k], m.h1[1].at[peer], "tensor", peer).wait_recv()
            value = m.hbox[0].astype(f32)
            for k in range(1, T):
                value += m.hbox[k].astype(f32)
            m.hsum[t] = value.astype(bf16)
            for k in range(1, T):
                hook_whole(k).start()

        produce_range(red_grad, 1, O, far_first, in_term, xs + own)
        scores.wait()
        ratios = scores.total()[0:1]
        loss = jnp.zeros((1, 1), f32)
        coefficients = jnp.zeros((1, LANES), f32)
        for k in range(S * D // 2):
            chosen, rejected = m.pairing[2 * k], m.pairing[2 * k + 1]
            margin = DPO_BETA * (
                jnp.sum(jnp.where(lane == chosen, ratios, 0.0), axis=1, keepdims=True)
                - jnp.sum(jnp.where(lane == rejected, ratios, 0.0), axis=1, keepdims=True)
            )
            soft = jnp.exp(-jnp.abs(margin))
            loss += jnp.maximum(-margin, 0.0) + jnp.log1p(soft)
            sigmoid = jnp.where(margin > 0, soft, 1.0) / (1.0 + soft)
            pull = DPO_BETA * LOSS_SCALE * sigmoid
            coefficients += jnp.where(lane == rejected, pull, 0.0) - jnp.where(
                lane == chosen, pull, 0.0
            )
        m.dpo_loss[...] = jnp.broadcast_to(loss, (8, LANES))
        own_coef = []
        for s in range(S):
            value = jnp.sum(jnp.where(lane == d * S + s, coefficients, 0.0), axis=1, keepdims=True)
            own_coef.append(value)
            m.ccol[s * L : (s + 1) * L, :] = jnp.broadcast_to(value, (L, 1))

        parts_q = jnp.zeros((z.rank, QC), f32)
        parts_v = jnp.zeros((z.rank, KC), f32)
        for s in range(S):
            rows = slice(s * L, (s + 1) * L)
            low = m.low[rows, :]
            parts_q += own_coef[s] * dot(low, m.dcat[rows, 0:QC], TN)[0 : z.rank]
            parts_v += own_coef[s] * dot(low, m.dcat[rows, QC + KC : NC], TN)[z.rank :]
        factors = exchange(m.fac, D, "dp", d)
        factors.own[:, 0:QC] = (ADAPTER_SCALE * parts_q).astype(bf16)
        factors.own[:, QC:] = (ADAPTER_SCALE * parts_v).astype(bf16)
        factors.box[d] = factors.own[...]
        factors.start()
        collect_range(red_grad, 0, 1, far_first)

        for k in range(1, T):
            peer = lax.rem(t + k, T)

            @pl.when(peer < z.HN)
            def _(peer=peer, k=k):
                slot = m.hsum.at[peer]
                remote(slot, slot, m.h2[0].at[k], m.h2[1].at[peer], "tensor", peer).wait_recv()

        hook = m.hsum[...].reshape(R, z.AR)
        hook = (hook.astype(f32) * m.ccol[...]).astype(bf16)
        adapters = exchange(m.ad, D, "dp", d)

        @pl.loop(0, T)
        def _(slot):
            ws, off = lax.div(slot, z.r), lax.rem(slot, z.r) * PW
            adapters.own[ws, pl.ds(pl.multiple_of(off, 16), PW), :] = dot(
                normed[slot, 0:R, :], hook, TN
            ).astype(bf16)

        adapters.box[d] = adapters.own[d]
        adapters.start()
        collect_range(red_grad, 1, O, far_first)
        m.pcol[0:R, :] = to_column(post2)
        finish(1, m.reference_out)
        stats3.wait()
        m.pcol[0:R, :] = to_column(stats3.total()[0:1])
        factors.wait()
        value = factors.total()
        m.query_factor_gradient[...] = value[:, 0:QC]
        m.value_factor_gradient[...] = value[:, QC:]
        red_grad.collect(a)

        pre_gain = m.gains[pl.ds(t, 1), :]

        def grad_in(rows):
            read = m.readout[rows, :].astype(f32) * m.liv[rows, :]
            scale = m.scol[rows, :]
            h = held[t, rows, :].astype(f32)
            value = (
                read
                + scale * pre_gain * m.gnorm[rows, :]
                - h * (scale * scale * m.pcol[rows, :] / z.W)
            )
            m.grad_hidden[rows, :] = (value * m.ccol[rows, :]).astype(bf16)

        chunks(grad_in)
        adapters.wait()

        def sum_adapters(rows):
            value = adapters.box[0, rows, :].astype(f32)
            for k in range(1, D):
                value += adapters.box[k, rows, :].astype(f32)
            m.grad_a[rows, :] = value

        size = pick(z.r * PW, (96, 48, 32, 16))

        @pl.loop(0, z.r * PW // size)
        def _(i):
            sum_adapters(pl.ds(pl.multiple_of(i * size, 16), size))

        hid[0].drain()
        hid[1].drain()
        gag.drain()
        red_ref.drain()
        red_grad.drain()
        weights_drain(wq)
        weights_drain(wo)
        for done in (stats0, stats1, stats2, stats3, scores, factors, adapters):
            done.drain()
        for k in range(1, T):
            peer = lax.rem(t + k, T)

            @pl.when(peer < z.HN)
            def _(peer=peer, k=k):
                hook_part(peer, k).wait_send()

        @pl.when(t < z.HN)
        def _():
            for k in range(1, T):
                hook_whole(k).wait_send()

    return kernel


def body(
    ref_hidden,
    pol_hidden,
    readout,
    lengths,
    pairing,
    pre_gain,
    post_gain,
    w_query,
    w_key,
    value_projection,
    w_out,
    a_query,
    a_value,
    query_second_factor,
    value_second_factor,
):
    z = Sizes(
        pol_hidden.shape[0],
        pol_hidden.shape[1],
        lengths.shape[0],
        lax.axis_size("dp"),
        lax.axis_size("tensor"),
        w_query.shape[1],
        w_key.shape[1],
        query_second_factor.shape[0],
    )
    gains = jnp.concatenate([pre_gain.reshape(z.T, z.PW), post_gain.reshape(z.T, z.PW)], axis=0)
    a_both = jnp.concatenate([a_query, a_value], axis=1)
    cosine, sine = rope_tables(z.L)
    vmem = pl.BlockSpec(memory_space=pltpu.VMEM)
    smem = pl.BlockSpec(memory_space=pltpu.SMEM)
    hbm = pl.BlockSpec(memory_space=pl.ANY)
    inputs = dict(
        pol_hidden=(pol_hidden, hbm),
        ref_hidden=(ref_hidden, hbm),
        readout=(readout, vmem),
        lengths=(lengths, smem),
        pairing=(pairing, smem),
        gains=(gains, vmem),
        w_query=(w_query, hbm),
        w_key=(w_key, hbm),
        value_projection=(value_projection, hbm),
        w_out=(w_out, hbm),
        a_both=(a_both, hbm),
        query_second_factor=(query_second_factor, vmem),
        value_second_factor=(value_second_factor, vmem),
        cosine=(jnp.asarray(cosine), vmem),
        sine=(jnp.asarray(sine), vmem),
    )
    outputs = dict(
        policy_out=((z.R, z.PW), bf16),
        reference_out=((z.R, z.PW), bf16),
        dpo_loss=((8, LANES), f32),
        grad_hidden=((z.R, z.PW), bf16),
        grad_a=((z.r * z.PW, z.AR), f32),
        query_factor_gradient=((z.rank, z.QC), f32),
        value_factor_gradient=((z.rank, z.KC), f32),
    )
    scratch = build_scratch(z)
    outs = pl.pallas_call(
        make_kernel(z, [*inputs, *outputs], scratch),
        name="preference_step",
        out_shape=[jax.ShapeDtypeStruct(*entry) for entry in outputs.values()],
        in_specs=[spec for _, spec in inputs.values()],
        out_specs=[vmem] * len(outputs),
        scratch_shapes=jax.tree.leaves(scratch),
        compiler_params=pltpu.CompilerParams(
            collective_id=1, has_side_effects=True, vmem_limit_bytes=VMEM_GRANT
        ),
    )(*[array for array, _ in inputs.values()])
    policy_out, reference_out, loss, grad_hidden, grad_a, grad_q, grad_v = outs
    return policy_out, reference_out, loss[0, 0], grad_hidden, grad_a, grad_q, grad_v


def solution(mesh):
    placed = (
        P("dp", "tensor"),
        P("dp", "tensor"),
        P("dp", "tensor"),
        P("dp"),
        P(),
        P(),
        P(),
        P("dp", "tensor"),
        P("dp", "tensor"),
        P("dp", "tensor"),
        P("dp", "tensor"),
        P("dp", None),
        P("dp", None),
        P(None, "tensor"),
        P(None, "tensor"),
    )
    return jax.shard_map(
        body,
        mesh=mesh,
        in_specs=placed,
        out_specs=(
            P("dp", "tensor"),
            P("dp", "tensor"),
            P(),
            P("dp", "tensor"),
            P("dp", None),
            P(None, "tensor"),
            P(None, "tensor"),
        ),
        check_vma=False,
    )
```

time: 410 us -> 257 us (0.63)
  Pallas kernels: 305 us -> 242 us
  matrix products: 51.2 us -> 0 us
  other arithmetic: 23.2 us -> 1.51 us
  local copies, waits for them, and re-layouts: 28.7 us -> 11.5 us
    pallas_call x8 -> x1, Pallas kernels: 305 us -> 242 us  [body(): pl.pallas_call(make_kernel(z, [*inputs, *outputs], scratch), name='prefer...]
    dot_general x23 -> x0, matrix products: 51.2 us -> none  [the longest x17 44.1 us: dot(): return lax.dot_general(a, b, dims, preferred_element_type=f32)]
    reduce_sum x11 -> x0, other arithmetic: 8.12 us -> none  [the longest x1 2.27 us: body(): jnp.sum(shaped * shaped, axis=2)]
    convert_element_type x9 -> x0, other arithmetic: 7.86 us -> none  [the longest x1 1.82 us: body(): grad_a = adapter_all.reshape(-1, adapter_all.shape[-1]).astype(f32)]
    dot_general x3 -> x0, local copies, waits for them, and re-layouts: 7.45 us -> none  [dot(): return lax.dot_general(a, b, dims, preferred_element_type=f32)]
    unnamed x57 -> x16, local copies, waits for them, and re-layouts: 4.77 us -> 8.66 us
where the time goes in v1:
time: 257 us; the launch traced here: 256 us
  Pallas kernels  242 us (94%)
  local copies, waits for them, and re-layouts  11.5 us (4%)
    pallas_call x1, Pallas kernels, body(): pl.pallas_call(make_kernel(z, [*inputs, *outputs], scratch), name='prefer...  242 us
    unnamed x16, local copies, waits for them, and re-layouts  8.66 us

profile of v1, /device:TPU:0, one launch (start us, length us, event | category | flops | bytes accessed | tf_op | source)
XLA Modules:
  0.0 255.6 jit_solution(12689843259071056643)
XLA Ops:
  0.6 0.8 reshape.20
  1.4 0.8 reshape.21
  2.2 0.6 pad_maximum_fusion.1.refs_5_
  2.9 1.1 copy.24
  4.0 1.1 copy.25
  5.1 0.9 pad_maximum_fusion.refs_10_
  6.0 241.9 %preference_step.1 = (bf16[288,576]{1,0:T(8,128)(2,1)}, bf16[288,576]{1,0:T(8,128)(2,1)}, f32[8,128]{1,0:T(8,128)}, bf16[288,576]{1,0:T(8,128)(2,1)}, f32[1152,1...) custom-call(bf16[288,576]{1,0:T(8,128)(2,1)} %refs_0_.1, bf16[288,576]{1,0:T(8,128)(2,1)} %refs_1_.1, ...), custom_call_target="tpu_custom_call" | custom-call | tf_op jit(solution)/shard_map/preference_step/pallas_call | solution.py:1142
  247.9 0.0 copy-start.1
  247.9 0.0 copy-start
  247.9 1.3 slice.3
  249.2 1.8 copy.32
  250.9 0.0 copy-start.2
  250.9 1.8 copy.33
  252.7 0.0 copy-done.1
  252.7 0.0 copy-start.3
  252.7 0.7 copy.34
  253.5 0.0 copy-done
  253.5 0.8 copy.35
  254.3 0.0 copy-done.2
  254.3 0.7 copy.36
  255.0 0.0 copy-done.3
  255.0 0.6 copy.37
Async XLA Ops:
  247.9 4.8 %copy-start.1 = (bf16[288,576]{1,0:T(8,128)(2,1)S(1)}, bf16[288,576]{1,0:T(8,128)(2,1)}, u32[]{:S(2)}) copy-start(bf16[288,576]{1,0:T(8,128)(2,1)} %get-tuple-element.31) | copy-start | bytes 995332
  247.9 5.6 %copy-start = (f32[1152,128]{1,0:T(8,128)S(1)}, f32[1152,128]{1,0:T(8,128)}, u32[]{:S(2)}) copy-start(f32[1152,128]{1,0:T(8,128)} %get-tuple-element.32) | copy-start | bytes 1769476
  250.9 3.4 %copy-start.2 = (f32[64,512]{1,0:T(8,128)S(1)}, f32[64,512]{1,0:T(8,128)}, u32[]{:S(2)}) copy-start(f32[64,512]{1,0:T(8,128)} %get-tuple-element.33) | copy-start | bytes 393220
  252.7 2.2 copy-start.3

commit v2 on v1

--- a/solution.py
+++ b/solution.py
@@ -170,7 +170,22 @@
         h2=sem(T, T),
         fac=[vm(D, z.rank, moved), vm(z.rank, moved)] + sem(D, D),
         ad=[vm(D, z.r * PW, z.AR), vm(D, z.r * PW, z.AR)] + sem(D, D),
-        load=sem(8),
+        load=sem(16),
+        emit=sem(8),
+        a_in=vm(2, z.r * PW, z.rank),
+        query_second_factor=vm(z.rank, z.QC),
+        value_second_factor=vm(z.rank, z.KC),
+        gains=vm(2 * T, PW, kind=f32),
+        readout=vm(R, PW),
+        cosine=vm(z.L, HEAD_SIZE, kind=f32),
+        sine=vm(z.L, HEAD_SIZE, kind=f32),
+        policy_out=vm(R, PW),
+        reference_out=vm(R, PW),
+        dpo_loss=vm(8, LANES, kind=f32),
+        grad_hidden=vm(R, PW),
+        grad_a=vm(z.r * PW, z.AR, kind=f32),
+        query_factor_gradient=vm(z.rank, z.QC, kind=f32),
+        value_factor_gradient=vm(z.rank, z.KC, kind=f32),
         hid=[gather_sems(n), gather_sems(n)],
         gag=gather_sems(n),
         wq=weight_sems(),
@@ -430,6 +445,13 @@
             def _(i):
                 fn(pl.ds(pl.multiple_of(i * z.step, 16), z.step))
 
+        emitted = []
+
+        def emit(ref, out):
+            copy = pltpu.make_async_copy(ref, out, m.emit[0].at[len(emitted)])
+            copy.start()
+            emitted.append(copy)
+
         def exchange(refs, count=T, axis="tensor", rank=t):
             return Exchange(axis, rank, count, *refs)
 
@@ -439,8 +461,16 @@
             (m.w_query, W.at[d, :, pl.ds(0, QC)]),
             (m.w_key, W.at[d, :, pl.ds(QC, KC)]),
             (m.value_projection, W.at[d, :, pl.ds(QC + KC, KC)]),
-            (m.a_both, W.at[d, :, pl.ds(NC, z.AR)]),
+            (m.a_query, m.a_in.at[0]),
+            (m.a_value, m.a_in.at[1]),
             (m.w_out, WO.at[d]),
+            (m.query_factor_hbm, m.query_second_factor),
+            (m.value_factor_hbm, m.value_second_factor),
+            (m.pre_rows, m.gains.at[pl.ds(0, T)]),
+            (m.post_rows, m.gains.at[pl.ds(T, T)]),
+            (m.readout_hbm, m.readout),
+            (m.cosine_hbm, m.cosine),
+            (m.sine_hbm, m.sine),
         ]
         copies = [
             pltpu.make_async_copy(src, dst, m.load[0].at[i]) for i, (src, dst) in enumerate(loads)
@@ -459,9 +489,6 @@
             )
 
         acc[...] = jnp.zeros_like(acc)
-        m.F[...] = jnp.zeros_like(m.F)
-        m.F[0 : z.rank, 0:QC] = m.query_second_factor[...]
-        m.F[z.rank :, QC:] = m.value_second_factor[...]
         for s in range(S):
             slot = lax.broadcasted_iota(jnp.int32, (L, 1), 0)
             m.liv[s * L : (s + 1) * L, :] = (slot < m.lengths[s]).astype(f32)
@@ -527,11 +554,23 @@
                         weight_copy(job, yy * C + core, order_of(q), k, False).wait_send()
 
         wq, wo = (W, m.wq), (WO, m.wo)
-        for copy in copies[2:6]:
+        for copy in copies[2:7]:
             copy.wait()
+        size = pick(z.r * PW, (96, 48, 32, 16))
+
+        @pl.loop(0, z.r * PW // size)
+        def _(i):
+            at = pl.ds(pl.multiple_of(i * size, 16), size)
+            W[d, at, NC:NW] = jnp.concatenate([m.a_in[0, at, :], m.a_in[1, at, :]], axis=1)
+
         weights_start(wq)
-        copies[6].wait()
+        copies[7].wait()
         weights_start(wo)
+        for copy in copies[8:]:
+            copy.wait()
+        m.F[...] = jnp.zeros_like(m.F)
+        m.F[0 : z.rank, 0:QC] = m.query_second_factor[...]
+        m.F[z.rank :, QC:] = m.value_second_factor[...]
 
         stats0.wait()
 
@@ -608,10 +647,7 @@
             for jj in range(1, Y):
                 weights_wait_core(wq, lax.rem(y + jj, Y), q)
 
-        @pl.loop(1, O)
-        def _(j):
-            hid[1].relay(visit(j))
-
+        hid[1].relay(visit(1))
         arrive(0, visit(O - 1))
         project_group(0, visit(O - 1), [0])
 
@@ -619,10 +655,14 @@
         def _(j):
             project_group(0, j, [1])
 
-        @pl.loop(0, O - 1)
+        @pl.loop(2, O)
         def _(j):
-            arrive(1, visit(j))
-            project_group(1, visit(j), [0, 1])
+            hid[1].relay(visit(j))
+
+        @pl.when(side > 0)
+        def _():
+            arrive(1, visit(0))
+            project_group(1, visit(0), [0, 1])
 
         weights_relay(wq, z.r - 1)
         for jj in range(1, Y):
@@ -725,41 +765,70 @@
                 for k in ks:
                     red.produce(order(j), k, term)
 
-        def collect_range(red, first, last, order):
+        def collect_stage(red, j, order, distance=None):
+            aa = order(j)
+            ahead = jnp.where(aa > a, a, O - 1 - a)
+            wanted = aa != a if distance is None else (aa != a) & (ahead == distance)
+
+            @pl.when(wanted)
+            def _():
+                red.collect(aa)
+
+        def collect_range(red, first, last, order, distance=None):
             @pl.loop(first, last)
             def _(j):
-                @pl.when(order(j) != a)
-                def _():
-                    red.collect(order(j))
+                collect_stage(red, j, order, distance)
 
         xs, own = list(range(1, I)), [0]
         for q in range(z.r):
             weights_wait_core(wo, y, q)
         produce_range(red_pol, 0, z.gp, near_first, out_term(0), xs + own)
-
-        arrive(1, visit(O - 1))
-        project_group(1, visit(O - 1), [0, 1])
-
-        @pl.loop(0, O)
-        def _(j):
-            project_group(1, j, [2])
-
-        attend(1)
-        collect_range(red_pol, 0, z.gp, near_first)
         early = z.r if I != z.r else z.r - 1
         for q in range(early):
             weights_relay(wo, q)
             for jj in range(1, Y):
                 weights_wait_core(wo, lax.rem(y + jj, Y), q)
         produce_range(red_pol, z.gp, O, near_first, out_term(0), xs)
+
+        @pl.loop(0, O)
+        def _(j):
+            @pl.when((j > 0) | (side == 0))
+            def _():
+                arrive(1, visit(j))
+                project_group(1, visit(j), [0, 1])
+
+            @pl.when(j == 1)
+            def _():
+                collect_range(red_pol, 0, 1, near_first, 0)
+
+        collect_range(red_pol, 1, z.gp, near_first, 0)
         for q in range(early, z.r):
             weights_relay(wo, q)
+
+        for q in range(early, z.r):
             for jj in range(1, Y):
                 weights_wait_core(wo, lax.rem(y + jj, Y), q)
         produce_range(red_pol, z.gp, O, near_first, out_term(0), own)
-        produce_range(red_ref, 0, 1, far_first, out_term(1), xs + own)
-        collect_range(red_pol, z.gp, O, near_first)
-        produce_range(red_ref, 1, 2, far_first, out_term(1), xs + own)
+        collect_range(red_pol, 0, z.gp, near_first, 1)
+        collect_range(red_pol, z.gp, z.gp + 1, near_first, 0)
+
+        @pl.loop(0, O)
+        def _(j):
+            project_group(1, j, [2])
+
+        attend(1)
+        produce_range(red_ref, 0, 2, far_first, out_term(1), xs + own)
+
+        for distance in range(2, O - 1):
+            collect_range(red_pol, 0, z.gp, near_first, distance)
+
+        @pl.loop(1, O - 1 + 2 * (O - 1 - z.gp))
+        def _(turn):
+            @pl.loop(z.gp, O)
+            def _(j):
+                collect_stage(red_pol, j, near_first, turn - 2 * (j - z.gp))
+
+        produce_range(red_ref, 2, O - 1, far_first, out_term(1), xs + own)
         red_pol.collect(a)
 
         post_gain = m.gains[pl.ds(T + t, 1), :]
@@ -788,7 +857,7 @@
             return done
 
         stats1 = token_sums(0, m.s1)
-        produce_range(red_ref, 2, O, far_first, out_term(1), xs + own)
+        collect_range(red_ref, 0, 2, far_first, 0)
         stats1.wait()
         sums1 = stats1.total()
         post1 = lax.rsqrt(sums1[0:1] / z.W + NORM_EPS)
@@ -818,6 +887,7 @@
 
         m.pcol[0:R, :] = m.col[0:R, :]
         finish(0, m.policy_out)
+        emit(m.policy_out, m.out_policy)
         m.gm[...] = jnp.zeros_like(m.gm)
 
         def back_out(aa):
@@ -829,40 +899,20 @@
                     m.gheld[slot], WO[ws, pl.ds(pl.multiple_of(off, 16), PW), :]
                 )
 
-        collect_range(red_ref, 0, O - 1, far_first)
+        collect_range(red_ref, 2, O - 1, far_first, 0)
 
         @pl.loop(1, O)
         def _(j):
             gag.relay(visit(j))
-
-            @pl.when(j == O - 1)
-            def _():
-                red_ref.collect(a)
-
             gag.wait_inner(visit(j - 1))
             back_out(visit(j - 1))
 
-        stats2 = token_sums(1, m.s2)
+        produce_range(red_ref, O - 1, O, far_first, out_term(1), xs + own)
+        collect_range(red_ref, 0, O - 1, far_first, 1)
         gag.wait_inner(visit(O - 1))
         back_out(visit(O - 1))
-        stats2.wait()
-        sums2 = stats2.total()
-        post2 = lax.rsqrt(sums2[0:1] / z.W + NORM_EPS)
-
-        token_pol = sums1[2:3] + post1 * sums1[1:2]
-        token_ref = sums2[2:3] + post2 * sums2[1:2]
-        wide = lax.broadcasted_iota(jnp.int32, (1, z.Rp), 1)
-        mine = jnp.zeros((1, LANES), f32)
-        for s in range(S):
-            inside = (wide >= s * L) & (wide < s * L + m.lengths[s])
-            value = jnp.sum(jnp.where(inside, token_pol, 0.0), axis=1, keepdims=True) - jnp.sum(
-                jnp.where(inside, token_ref, 0.0), axis=1, keepdims=True
-            )
-            mine = jnp.where(lane == d * S + s, value, mine)
-        scores = exchange(m.score, D, "dp", d)
-        scores.own[...] = jnp.broadcast_to(mine, (8, LANES))
-        scores.box[d] = scores.own[...]
-        scores.start()
+        for distance in range(2, O - 1):
+            collect_range(red_ref, 0, O - 1, far_first, distance)
         m.gmb[...] = m.gm[...].astype(bf16)
 
         @pl.loop(0, S)
@@ -940,6 +990,9 @@
         stats3.start()
         red_pol.drain()
         produce_range(red_grad, 0, 1, far_first, in_term, xs + own)
+        red_ref.collect(a)
+        stats2 = token_sums(1, m.s2)
+        produce_range(red_grad, 1, 2, far_first, in_term, xs + own)
 
         @pl.when(t < z.HN)
         def _():
@@ -956,7 +1009,27 @@
             for k in range(1, T):
                 hook_whole(k).start()
 
-        produce_range(red_grad, 1, O, far_first, in_term, xs + own)
+        produce_range(red_grad, 2, O, far_first, in_term, xs + own)
+        collect_range(red_grad, 0, 1, far_first)
+        stats2.wait()
+        sums2 = stats2.total()
+        post2 = lax.rsqrt(sums2[0:1] / z.W + NORM_EPS)
+
+        token_pol = sums1[2:3] + post1 * sums1[1:2]
+        token_ref = sums2[2:3] + post2 * sums2[1:2]
+        wide = lax.broadcasted_iota(jnp.int32, (1, z.Rp), 1)
+        mine = jnp.zeros((1, LANES), f32)
+        for s in range(S):
+            inside = (wide >= s * L) & (wide < s * L + m.lengths[s])
+            value = jnp.sum(jnp.where(inside, token_pol, 0.0), axis=1, keepdims=True) - jnp.sum(
+                jnp.where(inside, token_ref, 0.0), axis=1, keepdims=True
+            )
+            mine = jnp.where(lane == d * S + s, value, mine)
+        scores = exchange(m.score, D, "dp", d)
+        scores.own[...] = jnp.broadcast_to(mine, (8, LANES))
+        scores.box[d] = scores.own[...]
+        scores.start()
+        collect_range(red_grad, 1, 2, far_first)
         scores.wait()
         ratios = scores.total()[0:1]
         loss = jnp.zeros((1, 1), f32)
@@ -975,6 +1048,7 @@
                 lane == chosen, pull, 0.0
             )
         m.dpo_loss[...] = jnp.broadcast_to(loss, (8, LANES))
+        emit(m.dpo_loss, m.out_loss)
         own_coef = []
         for s in range(S):
             value = jnp.sum(jnp.where(lane == d * S + s, coefficients, 0.0), axis=1, keepdims=True)
@@ -993,7 +1067,6 @@
         factors.own[:, QC:] = (ADAPTER_SCALE * parts_v).astype(bf16)
         factors.box[d] = factors.own[...]
         factors.start()
-        collect_range(red_grad, 0, 1, far_first)
 
         for k in range(1, T):
             peer = lax.rem(t + k, T)
@@ -1016,15 +1089,18 @@
 
         adapters.box[d] = adapters.own[d]
         adapters.start()
-        collect_range(red_grad, 1, O, far_first)
+        collect_range(red_grad, 2, O - 1, far_first)
         m.pcol[0:R, :] = to_column(post2)
         finish(1, m.reference_out)
+        emit(m.reference_out, m.out_reference)
         stats3.wait()
         m.pcol[0:R, :] = to_column(stats3.total()[0:1])
         factors.wait()
         value = factors.total()
         m.query_factor_gradient[...] = value[:, 0:QC]
         m.value_factor_gradient[...] = value[:, QC:]
+        emit(m.query_factor_gradient, m.out_query)
+        emit(m.value_factor_gradient, m.out_value)
         red_grad.collect(a)
 
         pre_gain = m.gains[pl.ds(t, 1), :]
@@ -1041,6 +1117,7 @@
             m.grad_hidden[rows, :] = (value * m.ccol[rows, :]).astype(bf16)
 
         chunks(grad_in)
+        emit(m.grad_hidden, m.out_hidden)
         adapters.wait()
 
         def sum_adapters(rows):
@@ -1049,11 +1126,11 @@
                 value += adapters.box[k, rows, :].astype(f32)
             m.grad_a[rows, :] = value
 
-        size = pick(z.r * PW, (96, 48, 32, 16))
-
         @pl.loop(0, z.r * PW // size)
         def _(i):
             sum_adapters(pl.ds(pl.multiple_of(i * size, 16), size))
+
+        emit(m.grad_a, m.out_adapter)
 
         hid[0].drain()
         hid[1].drain()
@@ -1076,7 +1153,46 @@
             for k in range(1, T):
                 hook_whole(k).wait_send()
 
+        for copy in emitted:
+            copy.wait()
+
     return kernel
+
+
+def hand_over(arrays):
+    count = len(arrays)
+    shapes = [array.shape if array.shape != (8, LANES) else (1, 1) for array in arrays]
+
+    def kernel(*refs):
+        ins, outs, held = refs[:count], refs[count : 2 * count], refs[2 * count : 3 * count]
+        came, left = refs[3 * count :]
+        arrivals = [
+            pltpu.make_async_copy(src, dst, came.at[i])
+            for i, (src, dst) in enumerate(zip(ins, held))
+        ]
+        for copy in arrivals:
+            copy.start()
+        exits = []
+        for i, copy in enumerate(arrivals):
+            copy.wait()
+            if shapes[i] == (1, 1):
+                outs[i][...] = held[i][0:1, 0:1]
+            else:
+                exits.append(pltpu.make_async_copy(held[i], outs[i], left.at[i]))
+                exits[-1].start()
+        for copy in exits:
+            copy.wait()
+
+    hbm = pl.BlockSpec(memory_space=pl.ANY)
+    return pl.pallas_call(
+        kernel,
+        name="hand_over",
+        out_shape=[jax.ShapeDtypeStruct(s, a.dtype) for s, a in zip(shapes, arrays)],
+        in_specs=[hbm] * count,
+        out_specs=[pl.BlockSpec(memory_space=pltpu.VMEM) if s == (1, 1) else hbm for s in shapes],
+        scratch_shapes=[pltpu.VMEM(a.shape, a.dtype) for a in arrays]
+        + [pltpu.SemaphoreType.DMA((count,)), pltpu.SemaphoreType.DMA((count,))],
+    )(*arrays)
 
 
 def body(
@@ -1106,51 +1222,50 @@
         w_key.shape[1],
         query_second_factor.shape[0],
     )
-    gains = jnp.concatenate([pre_gain.reshape(z.T, z.PW), post_gain.reshape(z.T, z.PW)], axis=0)
-    a_both = jnp.concatenate([a_query, a_value], axis=1)
     cosine, sine = rope_tables(z.L)
-    vmem = pl.BlockSpec(memory_space=pltpu.VMEM)
     smem = pl.BlockSpec(memory_space=pltpu.SMEM)
     hbm = pl.BlockSpec(memory_space=pl.ANY)
     inputs = dict(
-        pol_hidden=(pol_hidden, hbm),
-        ref_hidden=(ref_hidden, hbm),
-        readout=(readout, vmem),
-        lengths=(lengths, smem),
-        pairing=(pairing, smem),
-        gains=(gains, vmem),
-        w_query=(w_query, hbm),
-        w_key=(w_key, hbm),
-        value_projection=(value_projection, hbm),
-        w_out=(w_out, hbm),
-        a_both=(a_both, hbm),
-        query_second_factor=(query_second_factor, vmem),
-        value_second_factor=(value_second_factor, vmem),
-        cosine=(jnp.asarray(cosine), vmem),
-        sine=(jnp.asarray(sine), vmem),
+        pol_hidden=pol_hidden,
+        ref_hidden=ref_hidden,
+        readout_hbm=readout,
+        lengths=lengths,
+        pairing=pairing,
+        pre_rows=pre_gain.reshape(z.T, z.PW),
+        post_rows=post_gain.reshape(z.T, z.PW),
+        w_query=w_query,
+        w_key=w_key,
+        value_projection=value_projection,
+        w_out=w_out,
+        a_query=a_query,
+        a_value=a_value,
+        query_factor_hbm=query_second_factor,
+        value_factor_hbm=value_second_factor,
+        cosine_hbm=jnp.asarray(cosine),
+        sine_hbm=jnp.asarray(sine),
     )
     outputs = dict(
-        policy_out=((z.R, z.PW), bf16),
-        reference_out=((z.R, z.PW), bf16),
-        dpo_loss=((8, LANES), f32),
-        grad_hidden=((z.R, z.PW), bf16),
-        grad_a=((z.r * z.PW, z.AR), f32),
-        query_factor_gradient=((z.rank, z.QC), f32),
-        value_factor_gradient=((z.rank, z.KC), f32),
+        out_policy=((z.R, z.PW), bf16),
+        out_reference=((z.R, z.PW), bf16),
+        out_loss=((8, LANES), f32),
+        out_hidden=((z.R, z.PW), bf16),
+        out_adapter=((z.r * z.PW, z.AR), f32),
+        out_query=((z.rank, z.QC), f32),
+        out_value=((z.rank, z.KC), f32),
     )
     scratch = build_scratch(z)
     outs = pl.pallas_call(
         make_kernel(z, [*inputs, *outputs], scratch),
         name="preference_step",
         out_shape=[jax.ShapeDtypeStruct(*entry) for entry in outputs.values()],
-        in_specs=[spec for _, spec in inputs.values()],
-        out_specs=[vmem] * len(outputs),
+        in_specs=[smem if array.ndim == 1 else hbm for array in inputs.values()],
+        out_specs=[hbm] * len(outputs),
         scratch_shapes=jax.tree.leaves(scratch),
         compiler_params=pltpu.CompilerParams(
             collective_id=1, has_side_effects=True, vmem_limit_bytes=VMEM_GRANT
         ),
-    )(*[array for array, _ in inputs.values()])
-    policy_out, reference_out, loss, grad_hidden, grad_a, grad_q, grad_v = outs
+    )(*inputs.values())
+    policy_out, reference_out, loss, grad_hidden, grad_a, grad_q, grad_v = hand_over(outs)
     return policy_out, reference_out, loss[0, 0], grad_hidden, grad_a, grad_q, grad_v
 
 

time: 257 us -> 239 us (0.930)
  Pallas kernels: 242 us -> 228 us
  local copies, waits for them, and re-layouts: 11.5 us -> 6.4 us
    pallas_call x1, Pallas kernels: 242 us -> 225 us  [body(): pl.pallas_call(make_kernel(z, [*inputs, *outputs], scratch), name='prefer...]
    unnamed x16 -> x2, local copies, waits for them, and re-layouts: 8.66 us -> 3.59 us
    pallas_call x0 -> x1, Pallas kernels: none -> 2.9 us  [hand_over(): pl.pallas_call(kernel, name='hand_over', out_shape=[jax.ShapeDtypeStruct(...]
where the time goes in v2:
time: 239 us; the launch traced here: 235 us
  Pallas kernels  228 us (95%)
  local copies, waits for them, and re-layouts  6.4 us (3%)
    pallas_call x1, Pallas kernels, body(): pl.pallas_call(make_kernel(z, [*inputs, *outputs], scratch), name='prefer...  225 us

profile of v2, /device:TPU:0, one launch (start us, length us, event | category | flops | bytes accessed | tf_op | source)
XLA Modules:
  0.0 235.2 jit_solution(853483498512103679)
XLA Ops:
  0.6 1.4 reshape.20.refs_5_
  2.0 1.4 reshape.21.refs_6_
  3.4 1.8 copy.24.refs_11_
  5.2 1.8 copy.25.refs_12_
  7.0 225.1 %preference_step.1 = (bf16[288,576]{1,0:T(8,128)(2,1)}, bf16[288,576]{1,0:T(8,128)(2,1)}, f32[8,128]{1,0:T(8,128)}, bf16[288,576]{1,0:T(8,128)(2,1)}, f32[1152,1...) custom-call(bf16[288,576]{1,0:T(8,128)(2,1)} %refs_0_.1, bf16[288,576]{1,0:T(8,128)(2,1)} %refs_1_.1, ...), custom_call_target="tpu_custom_call" | custom-call | tf_op jit(solution)/shard_map/preference_step/pallas_call | solution.py:1257
  232.1 2.9 %hand_over.1 = (bf16[288,576]{1,0:T(8,128)(2,1)}, bf16[288,576]{1,0:T(8,128)(2,1)}, f32[1,1]{1,0:T(1,128)}, bf16[288,576]{1,0:T(8,128)(2,1)}, f32[1152,128]{1,0:...) custom-call(bf16[288,576]{1,0:T(8,128)(2,1)} %get-tuple-element.21.refs_0_, bf16[288,576]{1,0:T(8,128)(2,1)} %get-tuple-element.22.refs_1_, ...), custom_call_target="tpu_custom_call" | custom-call | tf_op jit(solution)/shard_map/hand_over/pallas_call | solution.py:1187

commit v3 on v2

--- a/solution.py
+++ b/solution.py
@@ -172,7 +172,7 @@
         ad=[vm(D, z.r * PW, z.AR), vm(D, z.r * PW, z.AR)] + sem(D, D),
         load=sem(16),
         emit=sem(8),
-        a_in=vm(2, z.r * PW, z.rank),
+        a_in=vm(z.AR, z.r * PW),
         query_second_factor=vm(z.rank, z.QC),
         value_second_factor=vm(z.rank, z.KC),
         gains=vm(2 * T, PW, kind=f32),
@@ -461,8 +461,8 @@
             (m.w_query, W.at[d, :, pl.ds(0, QC)]),
             (m.w_key, W.at[d, :, pl.ds(QC, KC)]),
             (m.value_projection, W.at[d, :, pl.ds(QC + KC, KC)]),
-            (m.a_query, m.a_in.at[0]),
-            (m.a_value, m.a_in.at[1]),
+            (m.a_query, m.a_in.at[pl.ds(0, z.rank)]),
+            (m.a_value, m.a_in.at[pl.ds(z.rank, z.rank)]),
             (m.w_out, WO.at[d]),
             (m.query_factor_hbm, m.query_second_factor),
             (m.value_factor_hbm, m.value_second_factor),
@@ -503,6 +503,13 @@
         chunks(square, 2 * R)
         stats0.own[...] = stack_rows([to_lanes(m.col[0:R]), to_lanes(m.col[R:])])
         stats0.box[t] = stats0.own[...]
+
+        copies[5].wait()
+        copies[6].wait()
+        same = lax.broadcasted_iota(jnp.int32, (z.AR, z.AR), 0) == lax.broadcasted_iota(
+            jnp.int32, (z.AR, z.AR), 1
+        )
+        W[d, :, NC:NW] = dot(m.a_in[...], same.astype(bf16), TN).astype(bf16)
         pl.semaphore_wait(barrier, T - 1 + D - 1)
         stats0.start()
 
@@ -554,15 +561,8 @@
                         weight_copy(job, yy * C + core, order_of(q), k, False).wait_send()
 
         wq, wo = (W, m.wq), (WO, m.wo)
-        for copy in copies[2:7]:
+        for copy in copies[2:5]:
             copy.wait()
-        size = pick(z.r * PW, (96, 48, 32, 16))
-
-        @pl.loop(0, z.r * PW // size)
-        def _(i):
-            at = pl.ds(pl.multiple_of(i * size, 16), size)
-            W[d, at, NC:NW] = jnp.concatenate([m.a_in[0, at, :], m.a_in[1, at, :]], axis=1)
-
         weights_start(wq)
         copies[7].wait()
         weights_start(wo)
@@ -629,7 +629,10 @@
         side = jnp.minimum(a, O - 1 - a)
 
         def visit(j):
-            inside = jnp.where(lax.rem(j, 2) == 1, a - lax.div(j + 1, 2), a + lax.div(j, 2))
+            turn = jnp.where(a <= O - 1 - a, 1, -1)
+            inside = jnp.where(
+                lax.rem(j, 2) == 1, a + turn * lax.div(j + 1, 2), a - turn * lax.div(j, 2)
+            )
             outside = jnp.where(a <= O - 1 - a, a + j - side, a - j + side)
             return jnp.where(j <= 2 * side, inside, outside)
 
@@ -790,7 +793,7 @@
                 weights_wait_core(wo, lax.rem(y + jj, Y), q)
         produce_range(red_pol, z.gp, O, near_first, out_term(0), xs)
 
-        @pl.loop(0, O)
+        @pl.loop(0, O - 1)
         def _(j):
             @pl.when((j > 0) | (side == 0))
             def _():
@@ -809,8 +812,10 @@
             for jj in range(1, Y):
                 weights_wait_core(wo, lax.rem(y + jj, Y), q)
         produce_range(red_pol, z.gp, O, near_first, out_term(0), own)
+        collect_range(red_pol, z.gp, z.gp + 1, near_first, 0)
         collect_range(red_pol, 0, z.gp, near_first, 1)
-        collect_range(red_pol, z.gp, z.gp + 1, near_first, 0)
+        arrive(1, visit(O - 1))
+        project_group(1, visit(O - 1), [0, 1])
 
         @pl.loop(0, O)
         def _(j):
@@ -828,7 +833,6 @@
             def _(j):
                 collect_stage(red_pol, j, near_first, turn - 2 * (j - z.gp))
 
-        produce_range(red_ref, 2, O - 1, far_first, out_term(1), xs + own)
         red_pol.collect(a)
 
         post_gain = m.gains[pl.ds(T + t, 1), :]
@@ -857,6 +861,7 @@
             return done
 
         stats1 = token_sums(0, m.s1)
+        produce_range(red_ref, 2, O - 1, far_first, out_term(1), xs + own)
         collect_range(red_ref, 0, 2, far_first, 0)
         stats1.wait()
         sums1 = stats1.total()
@@ -904,10 +909,14 @@
         @pl.loop(1, O)
         def _(j):
             gag.relay(visit(j))
+
+            @pl.when(j == O - 1)
+            def _():
+                produce_range(red_ref, O - 1, O, far_first, out_term(1), xs + own)
+
             gag.wait_inner(visit(j - 1))
             back_out(visit(j - 1))
 
-        produce_range(red_ref, O - 1, O, far_first, out_term(1), xs + own)
         collect_range(red_ref, 0, O - 1, far_first, 1)
         gag.wait_inner(visit(O - 1))
         back_out(visit(O - 1))
@@ -1009,8 +1018,9 @@
             for k in range(1, T):
                 hook_whole(k).start()
 
-        produce_range(red_grad, 2, O, far_first, in_term, xs + own)
+        produce_range(red_grad, 2, O - 1, far_first, in_term, xs + own)
         collect_range(red_grad, 0, 1, far_first)
+        produce_range(red_grad, O - 1, O, far_first, in_term, xs + own)
         stats2.wait()
         sums2 = stats2.total()
         post2 = lax.rsqrt(sums2[0:1] / z.W + NORM_EPS)
@@ -1029,7 +1039,6 @@
         scores.own[...] = jnp.broadcast_to(mine, (8, LANES))
         scores.box[d] = scores.own[...]
         scores.start()
-        collect_range(red_grad, 1, 2, far_first)
         scores.wait()
         ratios = scores.total()[0:1]
         loss = jnp.zeros((1, 1), f32)
@@ -1089,7 +1098,7 @@
 
         adapters.box[d] = adapters.own[d]
         adapters.start()
-        collect_range(red_grad, 2, O - 1, far_first)
+        collect_range(red_grad, 1, O - 1, far_first)
         m.pcol[0:R, :] = to_column(post2)
         finish(1, m.reference_out)
         emit(m.reference_out, m.out_reference)
@@ -1125,6 +1134,8 @@
             for k in range(1, D):
                 value += adapters.box[k, rows, :].astype(f32)
             m.grad_a[rows, :] = value
+
+        size = pick(z.r * PW, (96, 48, 32, 16))
 
         @pl.loop(0, z.r * PW // size)
         def _(i):
@@ -1237,8 +1248,8 @@
         w_key=w_key,
         value_projection=value_projection,
         w_out=w_out,
-        a_query=a_query,
-        a_value=a_value,
+        a_query=a_query.T,
+        a_value=a_value.T,
         query_factor_hbm=query_second_factor,
         value_factor_hbm=value_second_factor,
         cosine_hbm=jnp.asarray(cosine),

time: 239 us -> 230 us (0.962)
  Pallas kernels: 228 us -> 223 us
  local copies, waits for them, and re-layouts: 6.4 us -> 2.81 us
    pallas_call x1, Pallas kernels: 225 us -> 220 us  [body(): pl.pallas_call(make_kernel(z, [*inputs, *outputs], scratch), name='prefer...]
    unnamed x2 -> x0, local copies, waits for them, and re-layouts: 3.59 us -> none
where the time goes in v3:
time: 230 us; the launch traced here: 227 us
  Pallas kernels  223 us (97%)
  local copies, waits for them, and re-layouts  2.81 us (1%)
    pallas_call x1, Pallas kernels, body(): pl.pallas_call(make_kernel(z, [*inputs, *outputs], scratch), name='prefer...  220 us

profile of v3, /device:TPU:0, one launch (start us, length us, event | category | flops | bytes accessed | tf_op | source)
XLA Modules:
  0.0 226.9 jit_solution(15139341055671843139)
XLA Ops:
  0.6 1.4 reshape.20.refs_5_
  2.0 1.4 reshape.21.refs_6_
  3.4 220.4 %preference_step.1 = (bf16[288,576]{1,0:T(8,128)(2,1)}, bf16[288,576]{1,0:T(8,128)(2,1)}, f32[8,128]{1,0:T(8,128)}, bf16[288,576]{1,0:T(8,128)(2,1)}, f32[1152,1...) custom-call(bf16[288,576]{1,0:T(8,128)(2,1)} %refs_0_.1, bf16[288,576]{1,0:T(8,128)(2,1)} %refs_1_.1, ...), custom_call_target="tpu_custom_call" | custom-call | tf_op jit(solution)/shard_map/preference_step/pallas_call | solution.py:1268
  223.8 2.9 %hand_over.1 = (bf16[288,576]{1,0:T(8,128)(2,1)}, bf16[288,576]{1,0:T(8,128)(2,1)}, f32[1,1]{1,0:T(1,128)}, bf16[288,576]{1,0:T(8,128)(2,1)}, f32[1152,128]{1,0:...) custom-call(bf16[288,576]{1,0:T(8,128)(2,1)} %get-tuple-element.21.refs_0_, bf16[288,576]{1,0:T(8,128)(2,1)} %get-tuple-element.22.refs_1_, ...), custom_call_target="tpu_custom_call" | custom-call | tf_op jit(solution)/shard_map/hand_over/pallas_call | solution.py:1198
